TPU v7x, 128 devices: a whole 4x4x4 slice. The times are simulated.
128 devices in a mesh: chan: 4 (over y), tm: 32 (over z, x, core).
Axes of the slice: x: 4, y: 4, z: 4, core: 2. Of those that a mesh axis runs over, the one named last changes fastest.
Arguments:
- strain: float32 [768, 524288], P('chan', 'tm'), may hold values from -6 to 6
Outputs:
- power: float32 [768, 8192], P('chan', 'tm')
- nyquist: float32 [768], P('chan')
- mean_power: float32 [8192], P('tm')
All inputs are finite; a program needn't handle non-finite values.
Results may differ from a plain program's by a relative error of at most 0.00007.
Values sent between devices are 32-bit elements; how exact they have to be, the bound alone decides.
A program may use at most 192 MiB of HBM per device.

v0:
```python
import jax
import jax.numpy as jnp
from jax import lax
from jax.sharding import PartitionSpec as P

ROOT = 128


highest_mode = lax.Precision.HIGHEST


def shifted(block, axis, distance):
    devices = range(lax.axis_size(axis))
    route = [(i - distance, i) for i in devices if i - distance in devices]
    return lax.ppermute(block, axis, route)


def copy_for_each(array, axis):
    devices = lax.axis_size(axis)
    return lax.all_to_all(
        jnp.broadcast_to(array[None], (devices, *array.shape)), axis, 0, 0, tiled=True
    )


def over_copies(array, axis):
    everything = copy_for_each(array, axis)
    return jnp.sum(everything, axis=0)


def hann_window(seg_len):
    sample_pos = jnp.arange(seg_len, dtype=jnp.float32)
    return 0.5 - 0.5 * jnp.cos(2.0 * jnp.pi * sample_pos / seg_len)


def dft_tables(root_len):
    positions = jnp.arange(root_len, dtype=jnp.int32)
    products = positions[:, None] * positions[None, :]
    short_angle = 2.0 * jnp.pi * (products % root_len).astype(jnp.float32) / root_len
    long_angle = 2.0 * jnp.pi * products.astype(jnp.float32) / (root_len * root_len)
    half_root = root_len // 2
    parity = (1 - 2 * (positions % 2)).astype(jnp.float32)
    return (
        jnp.cos(short_angle),
        jnp.sin(short_angle),
        jnp.cos(long_angle),
        jnp.sin(long_angle),
        jnp.cos(short_angle[:half_root]),
        jnp.sin(short_angle[:half_root]),
        parity,
    )


def periodogram(pieces, tables, window):
    cos_short, sin_short, cos_long, sin_long, cos_half, sin_half, parity = tables
    root_len = cos_short.shape[0]
    piece_rows = pieces.shape[0]
    centred = (pieces - jnp.mean(pieces, axis=1, keepdims=True)) * window
    folded = centred.reshape(piece_rows, root_len, root_len)
    real_first = jnp.einsum("ka,rab->rkb", cos_short, folded, precision=highest_mode)
    imag_first = -jnp.einsum("ka,rab->rkb", sin_short, folded, precision=highest_mode)
    real_twist = real_first * cos_long + imag_first * sin_long
    imag_twist = imag_first * cos_long - real_first * sin_long
    real_final = jnp.einsum(
        "rkb,qb->rqk", real_twist, cos_half, precision=highest_mode
    ) + jnp.einsum("rkb,qb->rqk", imag_twist, sin_half, precision=highest_mode)
    imag_final = jnp.einsum(
        "rkb,qb->rqk", imag_twist, cos_half, precision=highest_mode
    ) - jnp.einsum("rkb,qb->rqk", real_twist, sin_half, precision=highest_mode)
    spectrum_power = (real_final * real_final + imag_final * imag_final).reshape(piece_rows, -1)
    edge_term = jnp.sum(folded * parity, axis=(1, 2))
    return (spectrum_power, edge_term * edge_term)


def per_device(strain):
    chan_rows, time_width = strain.shape
    seg_len = ROOT * ROOT
    half_len = seg_len // 2
    window = hann_window(seg_len)
    energy = jnp.sum(window * window)
    tables = dft_tables(ROOT)
    tm_count = lax.axis_size("tm")
    block_count = time_width // half_len
    segments = block_count * tm_count - 1
    band_width = half_len // tm_count
    follower = shifted(strain[:, :half_len], "tm", -1)
    extended = jnp.concatenate([strain, follower], axis=1)
    is_last = (lax.axis_index("tm") == tm_count - 1).astype(jnp.float32)
    running_total = jnp.zeros((chan_rows, half_len), jnp.float32)
    nyquist_part = jnp.zeros((chan_rows,), jnp.float32)
    for segment_index in range(block_count):
        start = segment_index * half_len
        spectrum_power, edge_term = periodogram(
            extended[:, start : start + seg_len], tables, window
        )
        if segment_index == block_count - 1:
            keep_factor = 1.0 - is_last
            spectrum_power = spectrum_power * keep_factor
            edge_term = edge_term * keep_factor
        running_total = running_total + spectrum_power
        nyquist_part = nyquist_part + edge_term
    band_total = lax.psum_scatter(running_total, "tm", scatter_dimension=1, tiled=True)
    edges_total = over_copies(nyquist_part, "tm")
    bin_index = lax.axis_index("tm") * band_width + jnp.arange(band_width, dtype=jnp.int32)
    doubling = jnp.where(bin_index == 0, 1.0, 2.0).astype(jnp.float32)
    power = band_total * doubling / (segments * energy)
    nyquist = edges_total / (segments * energy)
    channel_sum = over_copies(jnp.sum(power, axis=0), "chan")
    mean_power = channel_sum / (chan_rows * lax.axis_size("chan"))
    return (power, nyquist, mean_power)


def solution(mesh):
    in_specs = (P("chan", "tm"),)
    out_specs = (P("chan", "tm"), P("chan"), P("tm"))
    return jax.shard_map(
        per_device, mesh=mesh, in_specs=in_specs, out_specs=out_specs, check_vma=False
    )
```

profile of v0, /device:TPU:2, one launch (start us, length us, event | category | flops | bytes accessed | tf_op | source)
XLA Modules:
  0.0 477.5 jit_solution(821330667707972011)
XLA Ops:
  7.2 0.0 reduce-scatter.2.cloned.1.call-start
  7.2 6.1 %slice.25 = f32[192,8192]{1,0:T(8,128)} slice(f32[192,16384]{1,0:T(8,128)} %param.1), slice={[0:192], [0:8192]} | slice | bytes 12582912 | tf_op jit(solution)/shard_map/slice | solution.py:85
  13.3 1.9 collective-permute-start
  15.2 0.2 fusion.37
  15.4 0.1 copy.33
  15.5 0.2 fusion.36
  15.8 0.1 copy.35
  15.9 0.2 multiply_subtract_fusion
  16.2 67.8 %collective-permute-done = f32[192,8192]{1,0:T(8,128)} collective-permute-done((f32[192,8192]{1,0:T(8,128)}, f32[192,8192]{1,0:T(8,128)}, u32[]{:S(2)}, u32[]{:S(2)}) %collective-permute-start) | collective-permute-done | bytes 6291488 | tf_op jit(solution)/shard_map/ppermute | solution.py:15
  84.0 9.8 %fusion.74 = (f32[192]{0:T(256)S(1)}, f32[192]{0:T(256)S(1)}) fusion(f32[192,16384]{1,0:T(8,128)} %param.1, f32[192,8192]{1,0:T(8,128)} %collective-permute-done), kind=kLoop, calls=%fused_computation.93 | loop fusion | flops 9436800 | bytes 18875904 | tf_op jit(solution)/shard_map/reduce_sum | solution.py:57
  93.8 22.8 %multiply_reduce_fusion.1 = (f32[192]{0:T(256)S(1)}, f32[192]{0:T(256)S(1)}, f32[24,8,128,128]{3,1,2,0:T(8,128)}, f32[24,8,128,128]{3,1,2,0:T(8,128)}) fusion(f32[192,16384]{1,0:T(8,128)} %param.1, f32[16384]{0:T(1024)S(1)} %broadcast_bitcast_fusion, f32[16384]{0:T(1024)S(1)} %multiply_subtract_fusion, f32[192]{0:T(256)S(1)} %get-tuple-element.12, ...), kind=kLoop, calls=%fused_computation.14 | loop fusion | flops 28311168 | bytes 44174336 | tf_op jit(solution)/shard_map/reduce_sum | solution.py:70
  116.6 11.5 %copy.62 = f32[24,8,128,128]{3,2,1,0:T(8,128)} copy(f32[24,8,128,128]{3,1,2,0:T(8,128)} %get-tuple-element.10) | data formatting | bytes 25165824
  128.1 0.0 slice-start
  128.1 0.0 slice-start.1
  128.1 0.0 slice-start.2
  128.1 24.5 %fusion.30 = f32[192,128,128]{2,1,0:T(8,128)S(1)} fusion(f32[192,128,128]{2,1,0:T(8,128)} %bitcast.93), kind=kOutput, calls=%fused_computation.39 | convolution fusion | flops 4832067584 | bytes 25165824 | tf_op jit(solution)/shard_map/ka,rab->rkb/dot_general | solution.py:60
  152.7 0.0 slice-done
  152.7 0.0 slice-done.1
  152.7 0.0 slice-done.2
  152.7 23.6 %fusion.34 = f32[192,128,128]{2,1,0:T(8,128)} fusion(f32[192,128,128]{2,1,0:T(8,128)S(1)} %bitcast.96), kind=kOutput, calls=%fused_computation.43 | convolution fusion | flops 4832067584 | bytes 25165824 | tf_op jit(solution)/shard_map/ka,rab->rkb/dot_general | solution.py:59
  176.3 13.1 %fusion.10 = f32[64,192,128]{2,0,1:T(8,128)} fusion(f32[192,128,128]{2,1,0:T(8,128)} %fusion.34, f32[192,128,128]{2,1,0:T(8,128)S(1)} %fusion.30, f32[128,128]{0,1:T(8,128)S(1)} %copy.35, f32[128,128]{0,1:T(8,128)S(1)} %copy.33, f32[128,128]{1,0:T(8,128)S(1)} %fusion.27), kind=kOutput, calls=%fused_computation.23 | convolution fusion | flops 2428502016 | bytes 31621120 | tf_op jit(solution)/shard_map/rkb,qb->rqk/dot_general | solution.py:68
  189.4 13.2 %fusion.12 = f32[64,192,128]{2,0,1:T(8,128)} fusion(f32[192,128,128]{2,1,0:T(8,128)} %fusion.34, f32[192,128,128]{2,1,0:T(8,128)S(1)} %fusion.30, f32[128,128]{0,1:T(8,128)S(1)} %copy.35, f32[128,128]{0,1:T(8,128)S(1)} %copy.33, f32[128,128]{1,0:T(8,128)S(1)} %fusion.27), kind=kOutput, calls=%fused_computation.24 | convolution fusion | flops 2428502016 | bytes 31621120 | tf_op jit(solution)/shard_map/rkb,qb->rqk/dot_general | solution.py:63
  202.6 12.9 %fusion.6 = f32[64,192,128]{2,0,1:T(8,128)} fusion(f32[192,128,128]{2,1,0:T(8,128)} %fusion.34, f32[192,128,128]{2,1,0:T(8,128)S(1)} %fusion.30, f32[128,128]{0,1:T(8,128)S(1)} %copy.35, f32[128,128]{0,1:T(8,128)S(1)} %copy.33, f32[128,128]{1,0:T(8,128)S(1)} %fusion.27), kind=kOutput, calls=%fused_computation.21 | convolution fusion | flops 2428502016 | bytes 31621120 | tf_op jit(solution)/shard_map/rkb,qb->rqk/dot_general | solution.py:66
  215.6 12.9 %fusion.8 = f32[64,192,128]{2,0,1:T(8,128)} fusion(f32[192,128,128]{2,1,0:T(8,128)} %fusion.34, f32[192,128,128]{2,1,0:T(8,128)S(1)} %fusion.30, f32[128,128]{0,1:T(8,128)S(1)} %copy.35, f32[128,128]{0,1:T(8,128)S(1)} %copy.33, f32[128,128]{1,0:T(8,128)S(1)} %fusion.27), kind=kOutput, calls=%fused_computation.22 | convolution fusion | flops 2428502016 | bytes 31621120 | tf_op jit(solution)/shard_map/rkb,qb->rqk/dot_general | solution.py:65
  228.4 11.4 %copy.63 = f32[24,8,128,128]{3,2,1,0:T(8,128)} copy(f32[24,8,128,128]{3,1,2,0:T(8,128)} %get-tuple-element.9) | data formatting | bytes 25165824
  239.8 0.0 slice-start.3
  239.8 0.0 slice-start.4
  239.8 0.0 slice-start.5
  239.8 24.7 %fusion.28 = f32[192,128,128]{2,1,0:T(8,128)S(1)} fusion(f32[192,128,128]{2,1,0:T(8,128)} %bitcast.97), kind=kOutput, calls=%fused_computation.37 | convolution fusion | flops 4832067584 | bytes 25165824 | tf_op jit(solution)/shard_map/ka,rab->rkb/dot_general | solution.py:60
  264.5 0.0 slice-done.3
  264.5 0.0 slice-done.4
  264.5 0.0 slice-done.5
  264.6 0.0 copy-start
  264.6 23.5 %fusion.32 = f32[192,128,128]{2,1,0:T(8,128)} fusion(f32[192,128,128]{2,1,0:T(8,128)S(1)} %bitcast.100), kind=kOutput, calls=%fused_computation.41 | convolution fusion | flops 4832067584 | bytes 25165824 | tf_op jit(solution)/shard_map/ka,rab->rkb/dot_general | solution.py:59
  288.1 12.8 %fusion.16 = f32[64,192,128]{2,0,1:T(8,128)} fusion(f32[192,128,128]{2,1,0:T(8,128)} %fusion.32, f32[192,128,128]{2,1,0:T(8,128)S(1)} %fusion.28, f32[128,128]{0,1:T(8,128)S(1)} %copy.35, f32[128,128]{0,1:T(8,128)S(1)} %copy.33, f32[128,128]{1,0:T(8,128)S(1)} %fusion.27), kind=kOutput, calls=%fused_computation.26 | convolution fusion | flops 2428502016 | bytes 31621120 | tf_op jit(solution)/shard_map/rkb,qb->rqk/dot_general | solution.py:65
  301.0 13.3 %fusion.18 = f32[64,192,128]{2,0,1:T(8,128)} fusion(f32[192,128,128]{2,1,0:T(8,128)} %fusion.32, f32[192,128,128]{2,1,0:T(8,128)S(1)} %fusion.28, f32[128,128]{0,1:T(8,128)S(1)} %copy.35, f32[128,128]{0,1:T(8,128)S(1)} %copy.33, f32[128,128]{1,0:T(8,128)S(1)} %fusion.27), kind=kOutput, calls=%fused_computation.27 | convolution fusion | flops 2428502016 | bytes 31621120 | tf_op jit(solution)/shard_map/rkb,qb->rqk/dot_general | solution.py:68
  314.2 0.0 copy-done
  314.2 12.9 %fusion.14 = f32[64,192,128]{2,0,1:T(8,128)} fusion(f32[192,128,128]{2,1,0:T(8,128)} %fusion.32, f32[192,128,128]{2,1,0:T(8,128)S(1)} %fusion.28, f32[128,128]{0,1:T(8,128)S(1)} %copy.35, f32[128,128]{0,1:T(8,128)S(1)} %copy.33, f32[128,128]{1,0:T(8,128)S(1)} %fusion.27), kind=kOutput, calls=%fused_computation.25 | convolution fusion | flops 2428502016 | bytes 31621120 | tf_op jit(solution)/shard_map/rkb,qb->rqk/dot_general | solution.py:66
  327.1 28.2 %multiply_add_fusion = f32[64,192,128]{2,0,1:T(8,128)} fusion(f32[64,192,128]{2,0,1:T(8,128)} %fusion.14, f32[64,192,128]{2,0,1:T(8,128)} %fusion.18, f32[64,192,128]{2,0,1:T(8,128)} %fusion.16, f32[64,192,128]{2,0,1:T(8,128)} %fusion.6, f32[64,192,128]{2,0,1:T(8,128)} %fusion.10, f32[64,192,128]{2,0,1:T(8,128)} %fusion.12, f32[64,192,128]{2,0,1:T(8,128)} %fusion.8, ...), kind=kOutput, calls=%fused_computation.20 | convolution fusion | flops 2447376384 | bytes 75661312 | tf_op jit(solution)/shard_map/rkb,qb->rqk/dot_general | solution.py:63
  355.4 10.9 %copy.66 = f32[24,8,64,128]{3,1,2,0:T(8,128)} copy(f32[24,8,64,128]{3,2,1,0:T(8,128)} %bitcast.102) | data formatting | bytes 12582912
  366.3 0.0 reduce-scatter.2.cloned.1.call-update
  366.3 0.6 broadcast_in_dim.12
  367.0 11.5 %all-to-all-start = ((f32[32,1,192]{2,1,0:T(1,128)}), f32[32,1,192]{2,1,0:T(1,128)S(1)}, u32[]{:S(2)}, u32[]{:S(2)}) async-start(f32[32,1,192]{2,1,0:T(1,128)} %broadcast_in_dim.12), calls=%async_computation.1 | async-start | bytes 65536 | tf_op jit(solution)/shard_map/all_to_all | solution.py:20
  378.5 0.8 multiply_reduce_fusion.2
  380.0 4.7 all-to-all-done
  384.7 0.1 reduce_sum.77
  384.7 73.3 %reduce-scatter.2.cloned.1.call-done = f32[192,256]{1,0:T(8,128)} async-done(((f32[192,8192]{1,0:T(8,128)}), f32[192,256]{1,0:T(8,128)}) %reduce-scatter.2.cloned.1.call-update) | async-done | bytes 196624 | tf_op jit(solution)/shard_map/reduce_scatter | solution.py:101
  458.0 1.6 fusion.75
  459.6 0.6 broadcast_in_dim.13
  460.2 4.2 all-to-all-start.1
  464.5 0.6 broadcast_divide_fusion
  465.0 4.7 all-to-all-done.1
  469.8 0.6 broadcast_multiply_fusion
  (9 shorter events, 0.1 us)
Async XLA Ops:
  7.2 450.8 %reduce-scatter.2.cloned.1.call-start = ((), (), s32[]{:S(2)}) async-start(), calls=%async_computation.3 | async-start | bytes 6488064 | tf_op jit(solution)/shard_map/reduce_scatter | solution.py:101
  13.3 70.7 %collective-permute-start = (f32[192,8192]{1,0:T(8,128)}, f32[192,8192]{1,0:T(8,128)}, u32[]{:S(2)}, u32[]{:S(2)}) collective-permute-start(f32[192,8192]{1,0:T(8,128)} %slice.25), channel_id=1, source_target_pairs={{1,0},{2,1},{3,2},{4,3},{5,4},{6,5},{7,6},{8,7},{9,8},{10,9},{11,1... | collective-permute-start | bytes 18874376 | tf_op jit(solution)/shard_map/ppermute | solution.py:15
  128.1 24.5 %slice-start = ((s8[12582912]{0:T(1024)(128)(4,1)}), s8[4194304]{0:T(1024)(128)(4,1)S(1)}, s32[]{:S(2)}) async-start(s8[12582912]{0:T(1024)(128)(4,1)} %bitcast.94), calls=%async_computation.4 | async-start | bytes 8388608
  128.1 24.5 %slice-start.1 = ((s8[12582912]{0:T(1024)(128)(4,1)}), s8[4194304]{0:T(1024)(128)(4,1)S(1)}, s32[]{:S(2)}) async-start(s8[12582912]{0:T(1024)(128)(4,1)} %bitcast.94), calls=%async_computation.5 | async-start | bytes 8388608
  128.1 24.6 %slice-start.2 = ((s8[12582912]{0:T(1024)(128)(4,1)}), s8[4194304]{0:T(1024)(128)(4,1)S(1)}, s32[]{:S(2)}) async-start(s8[12582912]{0:T(1024)(128)(4,1)} %bitcast.94), calls=%async_computation.6 | async-start | bytes 8388608
  239.8 24.7 %slice-start.3 = ((s8[12582912]{0:T(1024)(128)(4,1)}), s8[4194304]{0:T(1024)(128)(4,1)S(1)}, s32[]{:S(2)}) async-start(s8[12582912]{0:T(1024)(128)(4,1)} %bitcast.98), calls=%async_computation.7 | async-start | bytes 8388608
  239.8 24.7 %slice-start.4 = ((s8[12582912]{0:T(1024)(128)(4,1)}), s8[4194304]{0:T(1024)(128)(4,1)S(1)}, s32[]{:S(2)}) async-start(s8[12582912]{0:T(1024)(128)(4,1)} %bitcast.98), calls=%async_computation.8 | async-start | bytes 8388608
  239.8 24.7 %slice-start.5 = ((s8[12582912]{0:T(1024)(128)(4,1)}), s8[4194304]{0:T(1024)(128)(4,1)S(1)}, s32[]{:S(2)}) async-start(s8[12582912]{0:T(1024)(128)(4,1)} %bitcast.98), calls=%async_computation.9 | async-start | bytes 8388608
  264.6 49.6 %copy-start = (f32[192,128,128]{2,1,0:T(8,128)}, f32[192,128,128]{2,1,0:T(8,128)S(1)}, u32[]{:S(2)}) copy-start(f32[192,128,128]{2,1,0:T(8,128)S(1)} %fusion.28) | copy-start | bytes 37748740
  367.0 17.7 %all-to-all-start = ((f32[32,1,192]{2,1,0:T(1,128)}), f32[32,1,192]{2,1,0:T(1,128)S(1)}, u32[]{:S(2)}, u32[]{:S(2)}) async-start(f32[32,1,192]{2,1,0:T(1,128)} %broadcast_in_dim.12), calls=%async_computation.1 | async-start | bytes 65536 | tf_op jit(solution)/shard_map/all_to_all | solution.py:20
  460.2 9.5 %all-to-all-start.1 = ((f32[4,1,256]{2,1,0:T(1,128)}), f32[4,1,256]{2,1,0:T(1,128)S(1)}, u32[]{:S(2)}, u32[]{:S(2)}) async-start(f32[4,1,256]{2,1,0:T(1,128)} %broadcast_in_dim.13), calls=%async_computation.2 | async-start | bytes 8192 | tf_op jit(solution)/shard_map/all_to_all | solution.py:20
Sparse Core Ops, SparseCore 0:
  366.4 91.5 reduce-scatter.1
where the time goes:
time: 485 us; the launch traced here: 477 us
  matrix products  216 us (45%)
  waiting for transfers between devices  151 us (31%)
  local copies, waits for them, and re-layouts  41.3 us (9%)
  other arithmetic  37.1 us (8%)
  starting transfers between devices  17.7 us (4%)
  between operations  15.2 us (3%)
    reduce_scatter x1, waiting for transfers between devices, per_device(): lax.psum_scatter(running_total, 'tm', scatter_dimension=1, tiled=True)  73.3 us
    ppermute x1, waiting for transfers between devices, shifted(): return lax.ppermute(block, axis, route)  67.8 us
    dot_general x2, matrix products, periodogram(): jnp.einsum('ka,rab->rkb', sin_short, folded, precision=highest_mode)  49.2 us
    dot_general x2, matrix products, periodogram(): jnp.einsum('ka,rab->rkb', cos_short, folded, precision=highest_mode)  47.1 us
    dot_general x2, matrix products, periodogram(): jnp.einsum('rkb,qb->rqk', real_twist, cos_half, precision=highest_mode)  41.5 us
    unnamed x17, local copies, waits for them, and re-layouts  33.8 us
    dot_general x2, matrix products, periodogram(): jnp.einsum('rkb,qb->rqk', real_twist, sin_half, precision=highest_mode)  26.4 us
    dot_general x2, matrix products, periodogram(): jnp.einsum('rkb,qb->rqk', imag_twist, cos_half, precision=highest_mode)  25.8 us
  transfers between devices with their start and end apart: 4, of which 4 were waited for; matrix products, arithmetic and copies ran while one was open for 1% of the time, Pallas kernels for 0%

commit v1 on v0

v1 whole, which is shorter than its diff:
```python
import functools

import jax
import jax.numpy as jnp
import numpy as np
from jax import lax
from jax.experimental import pallas as pl
from jax.experimental.pallas import tpu as pltpu
from jax.sharding import PartitionSpec as P

SEG = 16384
ROOT = 128
F32 = jnp.float32
BF16 = jnp.bfloat16
STRIDE = 8
CHUNK = 2


def split(values):
    high = values.astype(BF16)
    low = (values - high.astype(F32)).astype(BF16)
    return high, low


def split_np(values):
    high = values.astype(np.float32).astype(BF16)
    low = (values - high.astype(np.float64)).astype(np.float32).astype(BF16)
    return high, low


def lane_bins():
    lane = np.arange(ROOT)
    owner, part = lane // 4, lane % 4
    return np.where(part < 2, 2 * owner + part, 127 - 2 * owner - (part - 2))


def tables():
    turn = 2.0 * np.pi / ROOT
    a = np.arange(ROOT)
    k1 = np.arange(64)
    cos_rows = np.cos(turn * ((k1[:, None] * a) % ROOT))
    sin_rows = -np.sin(turn * ((k1[:, None] * a) % ROOT))
    sin_rows[0] = 1.0 - 2.0 * (a % 2)
    first = np.concatenate([cos_rows, sin_rows], 0)
    first_high, first_low = split_np(first)
    first_high = np.concatenate([first_high, first_high], 1)
    first_low = np.concatenate([first_low, first_low], 1)
    q = lane_bins()
    cos_q = np.cos(turn * ((a[:, None] * q) % ROOT))
    sin_q = np.sin(turn * ((a[:, None] * q) % ROOT))
    last = np.concatenate(
        [np.concatenate([cos_q, -sin_q], 1), np.concatenate([sin_q, cos_q], 1)], 0
    )
    last_high, last_low = split_np(last)
    long_turn = 2.0 * np.pi / SEG
    twist = long_turn * (k1[:, None] * a)
    cos_twist = np.cos(twist).astype(np.float32)
    sin_twist = np.sin(twist).astype(np.float32)
    mid = long_turn * 64 * a
    mid_twist = np.stack([np.cos(mid), np.sin(mid)] + [0 * mid] * 6).astype(np.float32)
    n = np.arange(SEG, dtype=np.float64)
    window = (0.5 - 0.5 * np.cos(2.0 * np.pi * n / SEG)).astype(np.float32)
    slot, kind, k = np.meshgrid(np.arange(2), np.arange(2), np.arange(64), indexing="ij")
    place = np.where(slot == 0, k, np.where(k == 0, 64, 128 - k)) + 128 * kind
    perm = np.zeros((256, 256), np.float32)
    perm[np.arange(256), place.reshape(-1)] = 1.0
    energy = float(np.sum(window.astype(np.float64) ** 2))
    return (
        [
            np.concatenate([first_high, first_low], 0),
            last_high,
            last_low,
            cos_twist,
            sin_twist,
            mid_twist,
            window.reshape(ROOT, ROOT),
            perm.astype(BF16),
        ],
        energy,
    )


def dot(a, b):
    return jnp.dot(a, b, preferred_element_type=F32)


def first_stage(blocks, start, segs, ch, tabs, mean_ref, mean_base, mid_ref, high_ref, low_ref, row0):
    t_ref, vh_ref, vl_ref, c_ref, s_ref, mid_tw, w_ref = tabs
    w0, w1 = w_ref[:64, :], w_ref[64:, :]
    row = lax.broadcasted_iota(jnp.int32, (8, 256), 0)
    for pair in range(segs // 2):
        highs, lows = [], []
        for s in (2 * pair, 2 * pair + 1):
            mean = mean_ref[pl.ds(mean_base + s * 8 + ch, 1), :]
            r0, b0, b1 = blocks, start + s * 512, start + s * 512 + 512
            x0 = (r0[pl.ds(b0 + ch, 64, STRIDE), :] - mean) * w0
            x1 = (r0[pl.ds(b1 + ch, 64, STRIDE), :] - mean) * w1
            high, low = split(jnp.concatenate([x0, x1], 0))
            highs.append(high)
            lows.append(low)
        x = jnp.concatenate(
            [jnp.concatenate(highs, 1), jnp.concatenate(lows, 1)], 0
        )
        both = dot(t_ref[...], x)
        d = both[:128] + both[128:]
        fr = d[:64]
        fi = jnp.concatenate([jnp.where(row == 0, 0.0, d[64:72]), d[72:]], 0)
        mid = d[64:65]
        c, s_ = c_ref[...], s_ref[...]
        for i in range(2):
            s = 2 * pair + i
            lanes = slice(i * ROOT, (i + 1) * ROOT)
            tr = fr[:, lanes] * c + fi[:, lanes] * s_
            ti = fi[:, lanes] * c - fr[:, lanes] * s_
            put = row0 + 64 * s
            high, low = split(jnp.concatenate([tr, ti], 1))
            high_ref[pl.ds(put, 64), :] = high
            low_ref[pl.ds(put, 64), :] = low
            m = mid[:, lanes]
            mid_ref[pl.ds(mean_base + s * 8 + ch, 1), :] = jnp.concatenate(
                [m * mid_tw[0:1, :], -m * mid_tw[1:2, :]], 1
            )


def squares(high, low, vh_ref, vl_ref):
    o = dot(high, vh_ref[...]) + dot(low, vh_ref[...]) + dot(high, vl_ref[...])
    return o[:, :ROOT] * o[:, :ROOT] + o[:, ROOT:] * o[:, ROOT:]


GROUPS = 6
HALF_ROWS = 512
ENTRY_ROWS = 5 * HALF_ROWS
SEGS = 4


def remote(src, dst, send, recv, axis, index):
    return pltpu.make_async_remote_copy(
        src_ref=src,
        dst_ref=dst,
        send_sem=send,
        recv_sem=recv,
        device_id={axis: index},
        device_id_type=pl.DeviceIdType.MESH,
    )


def twin(r):
    return r + 1 - 2 * lax.rem(r, 2)


def welch_kernel(scale, x_ref, *refs):
    tabs, perm_ref, refs = refs[:7], refs[7], refs[8:]
    power_out, edge_out, mean_out = refs[:3]
    (buf, mean_ref, mid_ref, high_ref, low_ref, pow_ref, zs, zr, xs, xr, allf) = refs[3:14]
    (edge_z, edge_x, edge_sum, mean_buf) = refs[14:18]
    (load_sem, pair_send, pair_recv, halo_send, halo_recv, z_send, z_recv) = refs[18:25]
    (x_send, x_recv, d_send, d_recv, e_send, e_recv, m_send, m_recv) = refs[25:]
    y = lax.axis_index("chan")
    t = lax.axis_index("tm")
    core = lax.rem(t, 2)
    chip = t // 2
    x = lax.rem(chip, 4)
    z = chip // 4
    other = 1 - core
    device = lambda zz, xx, cc: (zz * 4 + xx) * 2 + cc

    def entry(g, half):
        return (g * 2 + half) * ENTRY_ROWS

    def load(g, half):
        row = (12 * core + 6 * half + g) * 1024
        to = entry(g, half) + (2 * core + half) * HALF_ROWS
        return pltpu.make_async_copy(
            x_ref.at[pl.ds(row, 1024), :], buf.at[pl.ds(to, 1024), :], load_sem.at[g, half]
        )

    def pair(g, half):
        row = (12 * other + 6 * half + g) * 1024
        to = entry(g, half) + (2 * core + half) * HALF_ROWS
        return remote(
            x_ref.at[pl.ds(row, 1024), :],
            buf.at[pl.ds(to, 1024), :],
            pair_send.at[g, half],
            pair_recv.at[g, half],
            "tm",
            device(z, x, other),
        )

    def halo(g, h):
        row = (12 * h + 6 * core + g) * 1024 + core * HALF_ROWS
        to = entry(g, core) + other * 4 * HALF_ROWS
        target = lax.rem(chip + 2 * core - 1 + 16, 16)
        return remote(
            x_ref.at[pl.ds(row, HALF_ROWS), :],
            buf.at[pl.ds(to, HALF_ROWS), :],
            halo_send.at[g, h],
            halo_recv.at[g, core],
            "tm",
            target * 2 + h,
        )

    def halo_arrival(g, half):
        to = entry(g, half) + (1 - half) * 4 * HALF_ROWS
        return remote(
            x_ref.at[pl.ds(0, HALF_ROWS), :],
            buf.at[pl.ds(to, HALF_ROWS), :],
            halo_send.at[g, half],
            halo_recv.at[g, half],
            "tm",
            device(z, x, other),
        )

    def partners(r, way):
        if way == 0:
            return twin(r), 3 - r
        return 3 - r, twin(r)

    def z_copy(g, way, slot):
        near, far = partners(z, way)
        to = near if slot < 2 else far
        chunk = (near, partners(near, way)[1], far)[slot]
        return remote(
            zs.at[way, g, pl.ds(chunk * 32, 32), :],
            zr.at[way, g, slot],
            z_send.at[way, g, slot],
            z_recv.at[way, g, slot],
            "tm",
            device(to, x, core),
        )

    def x_copy(g, way, slot):
        near, far = partners(x, way)
        to = near if slot < 2 else far
        chunk = (near, partners(near, way)[1], far)[slot]
        return remote(
            xs.at[way, g, pl.ds(chunk * 8, 8), :],
            xr.at[way, g, slot],
            x_send.at[way, g, slot],
            x_recv.at[way, g, slot],
            "tm",
            device(z, to, core),
        )

    def d_copy(g, half_owner):
        rows = allf.at[half_owner, pl.ds(g * 64, 64), :]
        return remote(rows, rows, d_send.at[g], d_recv.at[g], "tm", device(z, x, other))

    def edge_copy(stage, step):
        if stage == 0:
            return remote(
                edge_z.at[0], edge_z.at[step], e_send.at[0, step], e_recv.at[0, step],
                "tm", device(lax.rem(z + step, 4), x, core),
            )
        if stage == 1:
            return remote(
                edge_x.at[0], edge_x.at[step], e_send.at[1, step], e_recv.at[1, step],
                "tm", device(z, lax.rem(x + step, 4), core),
            )
        return remote(
            edge_sum.at[0], edge_sum.at[1], e_send.at[2, 0], e_recv.at[2, 0],
            "tm", device(z, x, other),
        )

    def mean_copy(step):
        return remote(
            mean_buf.at[0], mean_buf.at[step], m_send.at[step], m_recv.at[step],
            "chan", lax.rem(y + step, 4),
        )

    def z_first(g):
        for slot in (1, 0):
            for way in range(2):
                z_copy(g, way, slot).start()

    def z_second(g):
        for way in range(2):
            far = partners(z, way)[1]
            z_copy(g, way, 1).wait_recv()
            rows = pl.ds(pl.multiple_of(far * 32, 32), 32)
            zs[way, g, rows, :] = zs[way, g, rows, :] + zr[way, g, 1]
            z_copy(g, way, 2).start()

    def x_first(g):
        for way in range(2):
            z_copy(g, way, 0).wait_recv()
            z_copy(g, way, 2).wait_recv()
            rows = pl.ds(pl.multiple_of(z * 32, 32), 32)
            xs[way, g] = zs[way, g, rows, :] + zr[way, g, 0] + zr[way, g, 2]
            x_copy(g, way, 1).start()
            x_copy(g, way, 0).start()

    def x_second(g):
        for way in range(2):
            far = partners(x, way)[1]
            x_copy(g, way, 1).wait_recv()
            rows = pl.ds(pl.multiple_of(far * 8, 8), 8)
            xs[way, g, rows, :] = xs[way, g, rows, :] + xr[way, g, 1]
            x_copy(g, way, 2).start()

    def to_pair(g):
        for way in range(2):
            x_copy(g, way, 0).wait_recv()
            x_copy(g, way, 2).wait_recv()
            rows = pl.ds(pl.multiple_of(x * 8, 8), 8)
            total = xs[way, g, rows, :] + xr[way, g, 0] + xr[way, g, 2]
            for i in range(4):
                at = pl.multiple_of(g * 64 + (way * 4 + i) * 8, 8)
                allf[core, pl.ds(at, 8), :] = total[:, i * ROOT : (i + 1) * ROOT]
        d_copy(g, core).start()

    lane = lax.broadcasted_iota(jnp.int32, (8, ROOT), 1)

    def compute(g):
        for half in range(2):
            load(g, half).wait()
            first = pl.multiple_of(entry(g, half), 8)
            pair_arrival(g, half).wait_recv()
            halo_arrival(g, half).wait_recv()
            sums = []
            for i in range(5):
                rows = buf[pl.ds(pl.multiple_of(first + i * HALF_ROWS, 8), HALF_ROWS), :]
                rows = rows.reshape(64, 8, ROOT)
                sums.append(jnp.sum(jnp.sum(rows, axis=0), axis=1, keepdims=True))
            base = half * 32
            for s in range(SEGS):
                mean = (sums[s] + sums[s + 1]) * (1.0 / SEG)
                mean_ref[base + s * 8 : base + s * 8 + 8, :] = jnp.broadcast_to(mean, (8, ROOT))
            absent = (chip == 15, 3) if half == 0 else (chip == 0, 0)
            for ch in range(8):
                first_stage(
                    buf, first, SEGS, ch, tabs, mean_ref, base, mid_ref, high_ref, low_ref, ch * 256
                )
            for c0 in range(0, 8, CHUNK):
                sl = slice(c0 * 256, (c0 + CHUNK) * 256)
                sq = squares(high_ref[sl, :], low_ref[sl, :], tabs[1], tabs[2])
                for ch in range(c0, c0 + CHUNK):
                    power = jnp.zeros((64, ROOT), F32)
                    for s in range(SEGS):
                        r = (ch - c0) * 256 + s * 64
                        sqs = sq[r : r + 64]
                        if s == absent[1]:
                            sqs = jnp.where(absent[0], 0.0, sqs)
                        power = power + sqs
                    at = ch * 128 + 64 * half
                    pow_ref[at : at + 64, :] = power
            sq = squares(*split(mid_ref[base : base + 32, :]), tabs[1], tabs[2])
            middle = jnp.zeros((8, ROOT), F32)
            for s in range(SEGS):
                sqs = sq[s * 8 : s * 8 + 8]
                if s == absent[1]:
                    sqs = jnp.where(absent[0], 0.0, sqs)
                middle = middle + sqs
            zero = pow_ref[pl.ds(64 * half, 8, 128), :]
            last = jnp.sum(jnp.where(lane == ROOT - 1, zero, 0.0), axis=1, keepdims=True)
            rows = slice(half * 8, half * 8 + 8)
            edge_z[0, rows, :] = jnp.where(
                lane == g, jnp.broadcast_to(last, (8, ROOT)), edge_z[0, rows, :]
            )
            pow_ref[pl.ds(64 * half, 8, 128), :] = jnp.where(lax.rem(lane, 4) >= 2, middle, zero)
        for i in range(8):
            block = pow_ref[i * 128 : (i + 1) * 128, :].T
            zs[i // 4, g, :, (i % 4) * ROOT : (i % 4 + 1) * ROOT] = block

    def pair_arrival(g, half):
        to = entry(g, half) + (2 * other + half) * HALF_ROWS
        return remote(
            x_ref.at[pl.ds(0, 1024), :],
            buf.at[pl.ds(to, 1024), :],
            pair_send.at[g, half],
            pair_recv.at[g, half],
            "tm",
            device(z, x, other),
        )

    for g in range(GROUPS):
        for half in range(2):
            load(g, half).start()
    barrier = pltpu.get_barrier_semaphore()
    peers = [("tm", device(z, x, other))]
    for step in (1, 15):
        for h in range(2):
            peers.append(("tm", lax.rem(chip + step, 16) * 2 + h))
    for step in (1, 2, 3):
        peers.append(("tm", device(lax.rem(z + step, 4), x, core)))
        peers.append(("tm", device(z, lax.rem(x + step, 4), core)))
        peers.append(("chan", lax.rem(y + step, 4)))
    for axis, index in peers:
        pl.semaphore_signal(
            barrier, inc=1, device_id={axis: index}, device_id_type=pl.DeviceIdType.MESH
        )
    pl.semaphore_wait(barrier, len(peers))
    for g in range(GROUPS):
        for half in range(2):
            pair(g, half).start()
        for h in range(2):
            halo(g, h).start()
    edge_z[0] = jnp.zeros((16, ROOT), F32)

    def step(g, carry):
        @pl.when(g < GROUPS)
        def _():
            compute(g)
            z_first(g)

        @pl.when(g == GROUPS - 1)
        def _():
            for s in (1, 2, 3):
                edge_copy(0, s).start()

        @pl.when((g >= 1) & (g < GROUPS + 1))
        def _():
            z_second(g - 1)

        @pl.when((g >= 2) & (g < GROUPS + 2))
        def _():
            x_first(g - 2)

        @pl.when((g >= 3) & (g < GROUPS + 3))
        def _():
            x_second(g - 3)

        @pl.when(g >= 4)
        def _():
            to_pair(g - 4)

        return carry

    lax.fori_loop(0, GROUPS + 4, step, 0)

    total = edge_z[0]
    for s in (1, 2, 3):
        edge_copy(0, s).wait_recv()
        total = total + edge_z[s]
    edge_x[0] = total
    for s in (1, 2, 3):
        edge_copy(1, s).start()

    for g in range(GROUPS):
        d_copy(g, other).wait_recv()
    lane_row = lax.broadcasted_iota(jnp.int32, (1, ROOT), 1)
    column = jnp.zeros((8, 256), F32)
    pieces = []
    for par in range(2):
        stacked = []
        for h in range(2):
            near = allf[h, pl.ds(4 * core + par, 48, 8), :]
            far = allf[h, pl.ds(4 * core + par + 2, 48, 8), :]
            stacked.append(jnp.concatenate([near, far], 1))
        value = jnp.concatenate(stacked, 0)
        high, rest = split(value)
        low = rest.astype(F32)
        rest = (value - high.astype(F32)) - low
        placed = dot(high, perm_ref[...]) + dot(low.astype(BF16), perm_ref[...])
        placed = placed + dot(rest.astype(BF16), perm_ref[...])
        factor = jnp.full((1, ROOT), 2.0 * scale, F32)
        if par == 0:
            factor = jnp.where((lane_row == 0) & (t == 0), scale, factor)
        for kind in range(2):
            out = placed[:, kind * ROOT : (kind + 1) * ROOT] * factor
            for h in range(2):
                at = h * 96 + kind * 48
                power_out[at : at + 48, par * ROOT : (par + 1) * ROOT] = out[h * 48 : h * 48 + 48]
            pieces.append(out)
    sums = []
    for par in range(2):
        both = pieces[2 * par] + pieces[2 * par + 1]
        sums.append(jnp.sum(both, axis=0, keepdims=True))
    mean_buf[0] = jnp.broadcast_to(jnp.concatenate(sums, 1), (8, 256))
    for s in (1, 2, 3):
        mean_copy(s).start()

    total = edge_x[0]
    for s in (1, 2, 3):
        edge_copy(1, s).wait_recv()
        total = total + edge_x[s]
    edge_sum[0] = total
    edge_copy(2, 0).start()

    def drain(g, carry):
        for way in range(2):
            for slot in range(3):
                z_copy(g, way, slot).wait_send()
                x_copy(g, way, slot).wait_send()
            pair(g, way).wait_send()
            halo(g, way).wait_send()
        d_copy(g, core).wait_send()
        return carry

    lax.fori_loop(0, GROUPS, drain, 0)
    for s in (1, 2, 3):
        edge_copy(0, s).wait_send()
        edge_copy(1, s).wait_send()
    edge_copy(2, 0).wait_recv()
    edge_copy(2, 0).wait_send()
    edge_out[core] = edge_sum[0] * scale
    edge_out[other] = edge_sum[1] * scale
    mean = mean_buf[0]
    for s in (1, 2, 3):
        mean_copy(s).wait_recv()
        mean = mean + mean_buf[s]
    mean_out[...] = mean * (1.0 / 768.0)
    for s in (1, 2, 3):
        mean_copy(s).wait_send()


def per_device(strain):
    rows = strain.shape[0]
    tabs_np, energy = tables()
    tabs = [jnp.asarray(t) for t in tabs_np]
    groups = rows // 8
    x4 = strain.reshape(groups, 8, ROOT, ROOT).transpose(0, 2, 1, 3)
    x2 = x4.reshape(groups * 1024, ROOT)
    vmem = pl.BlockSpec(memory_space=pltpu.VMEM)
    dma = pltpu.SemaphoreType.DMA
    power, edge, mean = pl.pallas_call(
        functools.partial(welch_kernel, 1.0 / (63.0 * energy)),
        out_shape=[
            jax.ShapeDtypeStruct((192, 256), F32),
            jax.ShapeDtypeStruct((2, 16, ROOT), F32),
            jax.ShapeDtypeStruct((8, 256), F32),
        ],
        in_specs=[pl.BlockSpec(memory_space=pl.ANY)] + [vmem] * len(tabs),
        out_specs=[vmem] * 3,
        scratch_shapes=[
            pltpu.VMEM((GROUPS * 2 * ENTRY_ROWS, ROOT), F32),
            pltpu.VMEM((64, ROOT), F32),
            pltpu.VMEM((64, 256), F32),
            pltpu.VMEM((2048, 256), BF16),
            pltpu.VMEM((2048, 256), BF16),
            pltpu.VMEM((1024, ROOT), F32),
            pltpu.VMEM((2, GROUPS, 128, 512), F32),
            pltpu.VMEM((2, GROUPS, 3, 32, 512), F32),
            pltpu.VMEM((2, GROUPS, 32, 512), F32),
            pltpu.VMEM((2, GROUPS, 3, 8, 512), F32),
            pltpu.VMEM((2, GROUPS * 64, ROOT), F32),
            pltpu.VMEM((4, 16, ROOT), F32),
            pltpu.VMEM((4, 16, ROOT), F32),
            pltpu.VMEM((2, 16, ROOT), F32),
            pltpu.VMEM((4, 8, 256), F32),
            dma((GROUPS, 2)),
            dma((GROUPS, 2)),
            dma((GROUPS, 2)),
            dma((GROUPS, 2)),
            dma((GROUPS, 2)),
            dma((2, GROUPS, 3)),
            dma((2, GROUPS, 3)),
            dma((2, GROUPS, 3)),
            dma((2, GROUPS, 3)),
            dma((GROUPS,)),
            dma((GROUPS,)),
            dma((3, 4)),
            dma((3, 4)),
            dma((4,)),
            dma((4,)),
        ],
        compiler_params=pltpu.CompilerParams(
            collective_id=0, has_side_effects=True, vmem_limit_bytes=60 * 1024 * 1024
        ),
    )(x2, *tabs)
    nyquist = edge.reshape(2, 2, 8, ROOT)[..., :GROUPS].transpose(0, 1, 3, 2).reshape(rows)
    return power, nyquist, mean[0]


def solution(mesh):
    return jax.shard_map(
        per_device,
        mesh=mesh,
        in_specs=(P("chan", "tm"),),
        out_specs=(P("chan", "tm"), P("chan"), P("tm")),
        check_vma=False,
    )
```

time: 485 us -> 95.7 us (0.20); the launches traced: 477 us -> 94.3 us
  matrix products: 216 us -> 0 us
  waiting for transfers between devices: 151 us -> 0 us
  Pallas kernels: 0 us -> 89.3 us
  other arithmetic: 37.1 us -> 0 us
  local copies, waits for them, and re-layouts: 41.3 us -> 4.34 us
  starting transfers between devices: 17.7 us -> 0 us
  between operations: 15.2 us -> 0.64 us
    dot_general x12 -> x0, matrix products: 216 us -> none  [the longest x2 49.2 us: periodogram(): jnp.einsum('ka,rab->rkb', sin_short, folded, precision=highest_mode)]
    pallas_call x0 -> x1, Pallas kernels: none -> 89.3 us  [per_device(): pl.pallas_call(functools.partial(welch_kernel, 1.0 / (63.0 * energy)), ou...]
    reduce_scatter x1 -> x0, waiting for transfers between devices: 73.3 us -> none  [per_device(): lax.psum_scatter(running_total, 'tm', scatter_dimension=1, tiled=True)]
    ppermute x1 -> x0, waiting for transfers between devices: 67.8 us -> none  [shifted(): return lax.ppermute(block, axis, route)]
    reduce_sum x6 -> x0, other arithmetic: 35.2 us -> none  [the longest x1 22.8 us: periodogram(): edge_term = jnp.sum(folded * parity, axis=(1, 2))]
    unnamed x17 -> x2, local copies, waits for them, and re-layouts: 33.8 us -> 2.43 us
    all_to_all x2 -> x0, starting transfers between devices: 15.7 us -> none  [copy_for_each(): lax.all_to_all(jnp.broadcast_to(array[None], (devices, *array.shape)), ax...]
    all_to_all x2 -> x0, waiting for transfers between devices: 9.42 us -> none  [copy_for_each(): lax.all_to_all(jnp.broadcast_to(array[None], (devices, *array.shape)), ax...]
  transfers between devices with their start and end apart: 4 -> 0, of which waited for: 4 -> 0; matrix products, arithmetic and copies ran while one was open for 1% -> 0% of each run, Pallas kernels for 0% -> 0%
where the time goes in v1:
time: 95.7 us; the launch traced here: 94.3 us
  Pallas kernels  89.3 us (93%)
  local copies, waits for them, and re-layouts  4.34 us (5%)
    pallas_call x1, Pallas kernels, per_device(): pl.pallas_call(functools.partial(welch_kernel, 1.0 / (63.0 * energy)), ou...  89.3 us
    unnamed x2, local copies, waits for them, and re-layouts  2.43 us

profile of v1, /device:TPU:2, one launch (start us, length us, event | category | flops | bytes accessed | tf_op | source)
XLA Modules:
  0.0 94.3 jit_solution(11253114229974381364)
XLA Ops:
  0.6 89.3 %shard_map.112 = (f32[192,256]{1,0:T(8,128)}, f32[2,16,128]{2,1,0:T(8,128)}, f32[8,256]{1,0:T(8,128)}) custom-call(f32[24576,128]{1,0:T(8,128)} %bitcast.9, bf16[256,256]{1,0:T(8,128)(2,1)} %constant.16.clone.refs_0_, bf16[256,256]{1,0:T(8,128)(2,1)} %constant.17.clone.refs_1_, bf16[256,256]{1,0:T(8,128)(2,1)} %constant.18.clone.refs_2_, ...), custom_call_target="tpu_custom_call" | custom-call | tf_op jit(solution)/shard_map/pallas_call | solution.py:515
  89.9 0.8 copy.13
  90.7 0.7 reshape.21
  91.4 1.3 %slice.7 = f32[1,256]{1,0:T(1,128)} slice(f32[8,256]{1,0:T(8,128)} %get-tuple-element.8), slice={[0:1], [0:256]} | slice | bytes 2048 | tf_op jit(solution)/shard_map/slice | solution.py:561
  92.6 1.6 %copy.15 = f32[192,256]{1,0:T(8,128)} copy(f32[192,256]{1,0:T(8,128)} %get-tuple-element.12) | data formatting | bytes 393216

commit v2 on v1

--- a/solution.py
+++ b/solution.py
@@ -131,6 +131,8 @@
 HALF_ROWS = 512
 ENTRY_ROWS = 5 * HALF_ROWS
 SEGS = 4
+BATCHES = 3
+AHEAD = 2
 
 
 def remote(src, dst, send, recv, axis, index):
@@ -148,13 +150,31 @@
     return r + 1 - 2 * lax.rem(r, 2)
 
 
+def partners(r, way):
+    if way == 0:
+        return twin(r), 3 - r
+    return 3 - r, twin(r)
+
+
+def place(r, way):
+    if way == 0:
+        return lax.rem(2 * r - r // 2, 4)
+    return r
+
+
+def keep(r, way):
+    return place(r, way) // 2 * 2
+
+
 def welch_kernel(scale, x_ref, *refs):
     tabs, perm_ref, refs = refs[:7], refs[7], refs[8:]
     power_out, edge_out, mean_out = refs[:3]
-    (buf, mean_ref, mid_ref, high_ref, low_ref, pow_ref, zs, zr, xs, xr, allf) = refs[3:14]
-    (edge_z, edge_x, edge_sum, mean_buf) = refs[14:18]
-    (load_sem, pair_send, pair_recv, halo_send, halo_recv, z_send, z_recv) = refs[18:25]
-    (x_send, x_recv, d_send, d_recv, e_send, e_recv, m_send, m_recv) = refs[25:]
+    (relay, relay_send, relay_recv), refs = refs[3:6], refs[:3] + refs[6:]
+    (buf, mean_ref, mid_ref, high_ref, low_ref, pow_ref) = refs[3:9]
+    (zs, z_near, z_far, xs, x_near, x_far, allf) = refs[9:16]
+    (edge_z, edge_x, edge_sum, mean_buf) = refs[16:20]
+    (load_sem, pair_send, pair_recv, halo_send, halo_recv, z_send, z_recv) = refs[20:27]
+    (x_send, x_recv, d_send, d_recv, e_send, e_recv, m_send, m_recv) = refs[27:]
     y = lax.axis_index("chan")
     t = lax.axis_index("tm")
     core = lax.rem(t, 2)
@@ -186,64 +206,77 @@
             device(z, x, other),
         )
 
-    def halo(g, h):
-        row = (12 * h + 6 * core + g) * 1024 + core * HALF_ROWS
-        to = entry(g, core) + other * 4 * HALF_ROWS
-        target = lax.rem(chip + 2 * core - 1 + 16, 16)
-        return remote(
-            x_ref.at[pl.ds(row, HALF_ROWS), :],
-            buf.at[pl.ds(to, HALF_ROWS), :],
-            halo_send.at[g, h],
-            halo_recv.at[g, core],
-            "tm",
-            target * 2 + h,
-        )
-
-    def halo_arrival(g, half):
-        to = entry(g, half) + (1 - half) * 4 * HALF_ROWS
-        return remote(
-            x_ref.at[pl.ds(0, HALF_ROWS), :],
-            buf.at[pl.ds(to, HALF_ROWS), :],
+    def halo(g, half):
+        there = entry(g, half) + (1 - half) * 4 * HALF_ROWS
+        here = entry(g, half) + half * 4 * HALF_ROWS
+        target = lax.rem(chip + (15 if half == 0 else 1), 16)
+        return remote(
+            buf.at[pl.ds(here, HALF_ROWS), :],
+            buf.at[pl.ds(there, HALF_ROWS), :],
             halo_send.at[g, half],
             halo_recv.at[g, half],
             "tm",
-            device(z, x, other),
-        )
-
-    def partners(r, way):
-        if way == 0:
-            return twin(r), 3 - r
-        return 3 - r, twin(r)
-
-    def z_copy(g, way, slot):
+            target * 2 + core,
+        )
+
+    def hop(g, half):
+        here = entry(g, half) + half * 4 * HALF_ROWS
+        return remote(
+            buf.at[pl.ds(here, HALF_ROWS), :],
+            relay.at[pl.ds(g * HALF_ROWS, HALF_ROWS), :],
+            halo_send.at[g, half],
+            relay_recv.at[g],
+            "tm",
+            device(lax.rem(z + (3 if half == 0 else 1), 4), x, core),
+        )
+
+    def onward(g):
+        half = x // 3
+        there = entry(g, half) + (1 - half) * 4 * HALF_ROWS
+        return remote(
+            relay.at[pl.ds(g * HALF_ROWS, HALF_ROWS), :],
+            buf.at[pl.ds(there, HALF_ROWS), :],
+            relay_send.at[g],
+            halo_recv.at[g, half],
+            "tm",
+            device(z, 3 - x, core),
+        )
+
+    relays = (core == 1) & ((x == 0) | (x == 3))
+
+    def z_copy(g, way, step):
         near, far = partners(z, way)
-        to = near if slot < 2 else far
-        chunk = (near, partners(near, way)[1], far)[slot]
-        return remote(
-            zs.at[way, g, pl.ds(chunk * 32, 32), :],
-            zr.at[way, g, slot],
-            z_send.at[way, g, slot],
-            z_recv.at[way, g, slot],
+        if step == 0:
+            start, rows, into, to = (2 - keep(z, way)) * 32, 64, z_near, near
+        else:
+            start, rows, into, to = place(far, way) * 32, 32, z_far, far
+        return remote(
+            zs.at[way, g, pl.ds(start, rows), :],
+            into.at[way, g],
+            z_send.at[way, g, step],
+            z_recv.at[way, g, step],
             "tm",
             device(to, x, core),
         )
 
-    def x_copy(g, way, slot):
+    def x_copy(b, way, step):
         near, far = partners(x, way)
-        to = near if slot < 2 else far
-        chunk = (near, partners(near, way)[1], far)[slot]
-        return remote(
-            xs.at[way, g, pl.ds(chunk * 8, 8), :],
-            xr.at[way, g, slot],
-            x_send.at[way, g, slot],
-            x_recv.at[way, g, slot],
+        if step == 0:
+            start, size, into, to = 2 - keep(x, way), 2, x_near, near
+        else:
+            start, size, into, to = place(far, way), 1, x_far, far
+        return remote(
+            xs.at[way, b, pl.ds(start, size)],
+            into.at[way, b],
+            x_send.at[way, b, step],
+            x_recv.at[way, b, step],
             "tm",
             device(z, to, core),
         )
 
-    def d_copy(g, half_owner):
-        rows = allf.at[half_owner, pl.ds(g * 64, 64), :]
-        return remote(rows, rows, d_send.at[g], d_recv.at[g], "tm", device(z, x, other))
+    def d_copy(b, half_owner):
+        rows = allf.at[half_owner, pl.ds(b * 128, 128), :]
+        return remote(rows, rows, d_send.at[b], d_recv.at[b], "tm", device(z, x, other))
 
     def edge_copy(stage, step):
         if stage == 0:
@@ -268,54 +301,60 @@
         )
 
     def z_first(g):
-        for slot in (1, 0):
-            for way in range(2):
-                z_copy(g, way, slot).start()
+        for way in range(2):
+            z_copy(g, way, 0).start()
 
     def z_second(g):
         for way in range(2):
             far = partners(z, way)[1]
+            z_copy(g, way, 0).wait_recv()
+            at = place(far, way)
+            rows = pl.ds(pl.multiple_of(at * 32, 32), 32)
+            got = pl.ds(pl.multiple_of((at - keep(z, way)) * 32, 32), 32)
+            zs[way, g, rows, :] = zs[way, g, rows, :] + z_near[way, g, got, :]
+            z_copy(g, way, 1).start()
+
+    def z_last(g):
+        for way in range(2):
             z_copy(g, way, 1).wait_recv()
-            rows = pl.ds(pl.multiple_of(far * 32, 32), 32)
-            zs[way, g, rows, :] = zs[way, g, rows, :] + zr[way, g, 1]
-            z_copy(g, way, 2).start()
-
-    def x_first(g):
-        for way in range(2):
-            z_copy(g, way, 0).wait_recv()
-            z_copy(g, way, 2).wait_recv()
-            rows = pl.ds(pl.multiple_of(z * 32, 32), 32)
-            xs[way, g] = zs[way, g, rows, :] + zr[way, g, 0] + zr[way, g, 2]
-            x_copy(g, way, 1).start()
-            x_copy(g, way, 0).start()
-
-    def x_second(g):
+            at = place(z, way)
+            rows = pl.ds(pl.multiple_of(at * 32, 32), 32)
+            got = pl.ds(pl.multiple_of((at - keep(z, way)) * 32, 32), 32)
+            total = zs[way, g, rows, :] + z_near[way, g, got, :] + z_far[way, g]
+            for chunk in range(4):
+                spot = (0, 2, 3, 1)[chunk] if way == 0 else chunk
+                xs[way, g // 2, spot, lax.rem(g, 2)] = total[chunk * 8 : chunk * 8 + 8, :]
+
+    def x_first(b):
+        for way in range(2):
+            x_copy(b, way, 0).start()
+
+    def x_second(b):
         for way in range(2):
             far = partners(x, way)[1]
-            x_copy(g, way, 1).wait_recv()
-            rows = pl.ds(pl.multiple_of(far * 8, 8), 8)
-            xs[way, g, rows, :] = xs[way, g, rows, :] + xr[way, g, 1]
-            x_copy(g, way, 2).start()
-
-    def to_pair(g):
-        for way in range(2):
-            x_copy(g, way, 0).wait_recv()
-            x_copy(g, way, 2).wait_recv()
-            rows = pl.ds(pl.multiple_of(x * 8, 8), 8)
-            total = xs[way, g, rows, :] + xr[way, g, 0] + xr[way, g, 2]
-            for i in range(4):
-                at = pl.multiple_of(g * 64 + (way * 4 + i) * 8, 8)
-                allf[core, pl.ds(at, 8), :] = total[:, i * ROOT : (i + 1) * ROOT]
-        d_copy(g, core).start()
+            x_copy(b, way, 0).wait_recv()
+            at = place(far, way)
+            xs[way, b, at] = xs[way, b, at] + x_near[way, b, at - keep(x, way)]
+            x_copy(b, way, 1).start()
+
+    def to_pair(b):
+        for way in range(2):
+            x_copy(b, way, 1).wait_recv()
+            at = place(x, way)
+            total = xs[way, b, at] + x_near[way, b, at - keep(x, way)] + x_far[way, b, 0]
+            for k in range(2):
+                for i in range(4):
+                    row = pl.multiple_of(b * 128 + k * 64 + (way * 4 + i) * 8, 8)
+                    allf[core, pl.ds(row, 8), :] = total[k, :, i * ROOT : (i + 1) * ROOT]
+        d_copy(b, core).start()
 
     lane = lax.broadcasted_iota(jnp.int32, (8, ROOT), 1)
+    sub = lax.broadcasted_iota(jnp.int32, (8, ROOT), 0)
 
     def compute(g):
         for half in range(2):
-            load(g, half).wait()
             first = pl.multiple_of(entry(g, half), 8)
-            pair_arrival(g, half).wait_recv()
-            halo_arrival(g, half).wait_recv()
+            halo(g, half).wait_recv()
             sums = []
             for i in range(5):
                 rows = buf[pl.ds(pl.multiple_of(first + i * HALF_ROWS, 8), HALF_ROWS), :]
@@ -352,14 +391,15 @@
                 middle = middle + sqs
             zero = pow_ref[pl.ds(64 * half, 8, 128), :]
             last = jnp.sum(jnp.where(lane == ROOT - 1, zero, 0.0), axis=1, keepdims=True)
-            rows = slice(half * 8, half * 8 + 8)
-            edge_z[0, rows, :] = jnp.where(
-                lane == g, jnp.broadcast_to(last, (8, ROOT)), edge_z[0, rows, :]
-            )
+            spot = lane == 48 * half + 8 * g + sub
+            edge_z[0] = jnp.where(spot, jnp.broadcast_to(last, (8, ROOT)), edge_z[0])
             pow_ref[pl.ds(64 * half, 8, 128), :] = jnp.where(lax.rem(lane, 4) >= 2, middle, zero)
         for i in range(8):
             block = pow_ref[i * 128 : (i + 1) * 128, :].T
-            zs[i // 4, g, :, (i % 4) * ROOT : (i % 4 + 1) * ROOT] = block
+            lanes = slice((i % 4) * ROOT, (i % 4 + 1) * ROOT)
+            for chunk in range(4):
+                spot = ((0, 2, 3, 1)[chunk] if i < 4 else chunk) * 32
+                zs[i // 4, g, spot : spot + 32, lanes] = block[chunk * 32 : chunk * 32 + 32]
 
     def pair_arrival(g, half):
         to = entry(g, half) + (2 * other + half) * HALF_ROWS
@@ -378,8 +418,7 @@
     barrier = pltpu.get_barrier_semaphore()
     peers = [("tm", device(z, x, other))]
     for step in (1, 15):
-        for h in range(2):
-            peers.append(("tm", lax.rem(chip + step, 16) * 2 + h))
+        peers.append(("tm", lax.rem(chip + step, 16) * 2 + core))
     for step in (1, 2, 3):
         peers.append(("tm", device(lax.rem(z + step, 4), x, core)))
         peers.append(("tm", device(z, lax.rem(x + step, 4), core)))
@@ -389,14 +428,48 @@
             barrier, inc=1, device_id={axis: index}, device_id_type=pl.DeviceIdType.MESH
         )
     pl.semaphore_wait(barrier, len(peers))
-    for g in range(GROUPS):
+    def arrived(g):
+        for half in range(2):
+            load(g, half).wait()
+            pair_arrival(g, half).wait_recv()
+            by_relay = (core == 1) & (x == 3 * half)
+
+            @pl.when(by_relay)
+            def _():
+                hop(g, half).start()
+
+            @pl.when(jnp.logical_not(by_relay))
+            def _():
+                halo(g, half).start()
+
+    def forward(g):
+        @pl.when(relays)
+        def _():
+            hop(g, 0).wait_recv()
+            onward(g).start()
+
+    for g in range(AHEAD + 1):
         for half in range(2):
             pair(g, half).start()
-        for h in range(2):
-            halo(g, h).start()
-    edge_z[0] = jnp.zeros((16, ROOT), F32)
+    edge_z[0] = jnp.zeros((8, ROOT), F32)
+    for g in range(AHEAD):
+        arrived(g)
+    forward(0)
 
     def step(g, carry):
+        @pl.when(g < GROUPS - AHEAD - 1)
+        def _():
+            for half in range(2):
+                pair(g + AHEAD + 1, half).start()
+
+        @pl.when(g < GROUPS - AHEAD)
+        def _():
+            arrived(g + AHEAD)
+
+        @pl.when(g < GROUPS - 1)
+        def _():
+            forward(g + 1)
+
         @pl.when(g < GROUPS)
         def _():
             compute(g)
@@ -413,32 +486,45 @@
 
         @pl.when((g >= 2) & (g < GROUPS + 2))
         def _():
-            x_first(g - 2)
-
-        @pl.when((g >= 3) & (g < GROUPS + 3))
-        def _():
-            x_second(g - 3)
-
-        @pl.when(g >= 4)
-        def _():
-            to_pair(g - 4)
+            z_last(g - 2)
+
+        @pl.when((g >= 3) & (g < GROUPS + 2) & (lax.rem(g, 2) == 1))
+        def _():
+            x_first((g - 3) // 2)
+
+        @pl.when((g >= 4) & (g < GROUPS + 3) & (lax.rem(g, 2) == 0))
+        def _():
+            x_second((g - 4) // 2)
+
+        @pl.when((g >= 5) & (lax.rem(g, 2) == 1))
+        def _():
+            to_pair((g - 5) // 2)
+
+        @pl.when(g == GROUPS + 1)
+        def _():
+            total = edge_z[0]
+            for s in (1, 2, 3):
+                edge_copy(0, s).wait_recv()
+                total = total + edge_z[s]
+            edge_x[0] = total
+            for s in (1, 2, 3):
+                edge_copy(1, s).start()
+
+        @pl.when(g == GROUPS + 3)
+        def _():
+            total = edge_x[0]
+            for s in (1, 2, 3):
+                edge_copy(1, s).wait_recv()
+                total = total + edge_x[s]
+            edge_sum[0] = total
+            edge_copy(2, 0).start()
 
         return carry
 
     lax.fori_loop(0, GROUPS + 4, step, 0)
-
-    total = edge_z[0]
-    for s in (1, 2, 3):
-        edge_copy(0, s).wait_recv()
-        total = total + edge_z[s]
-    edge_x[0] = total
-    for s in (1, 2, 3):
-        edge_copy(1, s).start()
-
-    for g in range(GROUPS):
-        d_copy(g, other).wait_recv()
+    for b in range(BATCHES):
+        d_copy(b, other).wait_recv()
     lane_row = lax.broadcasted_iota(jnp.int32, (1, ROOT), 1)
-    column = jnp.zeros((8, 256), F32)
     pieces = []
     for par in range(2):
         stacked = []
@@ -469,36 +555,39 @@
     for s in (1, 2, 3):
         mean_copy(s).start()
 
-    total = edge_x[0]
-    for s in (1, 2, 3):
-        edge_copy(1, s).wait_recv()
-        total = total + edge_x[s]
-    edge_sum[0] = total
-    edge_copy(2, 0).start()
-
     def drain(g, carry):
         for way in range(2):
-            for slot in range(3):
-                z_copy(g, way, slot).wait_send()
-                x_copy(g, way, slot).wait_send()
+            for step in range(2):
+                z_copy(g, way, step).wait_send()
             pair(g, way).wait_send()
             halo(g, way).wait_send()
-        d_copy(g, core).wait_send()
+
+        @pl.when(relays)
+        def _():
+            onward(g).wait_send()
+
         return carry
 
     lax.fori_loop(0, GROUPS, drain, 0)
+    for b in range(BATCHES):
+        for way in range(2):
+            for step in range(2):
+                x_copy(b, way, step).wait_send()
+        d_copy(b, core).wait_send()
     for s in (1, 2, 3):
         edge_copy(0, s).wait_send()
         edge_copy(1, s).wait_send()
     edge_copy(2, 0).wait_recv()
     edge_copy(2, 0).wait_send()
-    edge_out[core] = edge_sum[0] * scale
-    edge_out[other] = edge_sum[1] * scale
+    for h in range(2):
+        mine = jnp.where(core == h, edge_sum[0], edge_sum[1])
+        row = jnp.sum(mine, axis=0, keepdims=True) * scale
+        edge_out[:, h * 96 : h * 96 + 96] = row[:, :96]
     mean = mean_buf[0]
     for s in (1, 2, 3):
         mean_copy(s).wait_recv()
         mean = mean + mean_buf[s]
-    mean_out[...] = mean * (1.0 / 768.0)
+    mean_out[...] = mean[:1] * (1.0 / 768.0)
     for s in (1, 2, 3):
         mean_copy(s).wait_send()
 
@@ -516,12 +605,15 @@
         functools.partial(welch_kernel, 1.0 / (63.0 * energy)),
         out_shape=[
             jax.ShapeDtypeStruct((192, 256), F32),
-            jax.ShapeDtypeStruct((2, 16, ROOT), F32),
-            jax.ShapeDtypeStruct((8, 256), F32),
+            jax.ShapeDtypeStruct((1, 192), F32),
+            jax.ShapeDtypeStruct((1, 256), F32),
         ],
         in_specs=[pl.BlockSpec(memory_space=pl.ANY)] + [vmem] * len(tabs),
         out_specs=[vmem] * 3,
         scratch_shapes=[
+            pltpu.VMEM((GROUPS * HALF_ROWS, ROOT), F32),
+            dma((GROUPS,)),
+            dma((GROUPS,)),
             pltpu.VMEM((GROUPS * 2 * ENTRY_ROWS, ROOT), F32),
             pltpu.VMEM((64, ROOT), F32),
             pltpu.VMEM((64, 256), F32),
@@ -529,25 +621,27 @@
             pltpu.VMEM((2048, 256), BF16),
             pltpu.VMEM((1024, ROOT), F32),
             pltpu.VMEM((2, GROUPS, 128, 512), F32),
-            pltpu.VMEM((2, GROUPS, 3, 32, 512), F32),
+            pltpu.VMEM((2, GROUPS, 64, 512), F32),
             pltpu.VMEM((2, GROUPS, 32, 512), F32),
-            pltpu.VMEM((2, GROUPS, 3, 8, 512), F32),
+            pltpu.VMEM((2, BATCHES, 4, 2, 8, 512), F32),
+            pltpu.VMEM((2, BATCHES, 2, 2, 8, 512), F32),
+            pltpu.VMEM((2, BATCHES, 1, 2, 8, 512), F32),
             pltpu.VMEM((2, GROUPS * 64, ROOT), F32),
-            pltpu.VMEM((4, 16, ROOT), F32),
-            pltpu.VMEM((4, 16, ROOT), F32),
-            pltpu.VMEM((2, 16, ROOT), F32),
+            pltpu.VMEM((4, 8, ROOT), F32),
+            pltpu.VMEM((4, 8, ROOT), F32),
+            pltpu.VMEM((2, 8, ROOT), F32),
             pltpu.VMEM((4, 8, 256), F32),
             dma((GROUPS, 2)),
             dma((GROUPS, 2)),
             dma((GROUPS, 2)),
             dma((GROUPS, 2)),
             dma((GROUPS, 2)),
-            dma((2, GROUPS, 3)),
-            dma((2, GROUPS, 3)),
-            dma((2, GROUPS, 3)),
-            dma((2, GROUPS, 3)),
-            dma((GROUPS,)),
-            dma((GROUPS,)),
+            dma((2, GROUPS, 2)),
+            dma((2, GROUPS, 2)),
+            dma((2, BATCHES, 2)),
+            dma((2, BATCHES, 2)),
+            dma((BATCHES,)),
+            dma((BATCHES,)),
             dma((3, 4)),
             dma((3, 4)),
             dma((4,)),
@@ -557,8 +651,8 @@
             collective_id=0, has_side_effects=True, vmem_limit_bytes=60 * 1024 * 1024
         ),
     )(x2, *tabs)
-    nyquist = edge.reshape(2, 2, 8, ROOT)[..., :GROUPS].transpose(0, 1, 3, 2).reshape(rows)
-    return power, nyquist, mean[0]
+    nyquist = edge.reshape(rows)
+    return power, nyquist, mean.reshape(256)
 
 
 def solution(mesh):

time: 95.7 us -> 82.9 us (0.87); the launches traced: 94.3 us -> 82.7 us
  Pallas kernels: 89.3 us -> 78.1 us
    pallas_call x1, Pallas kernels: 89.3 us -> 78.1 us  [per_device(): pl.pallas_call(functools.partial(welch_kernel, 1.0 / (63.0 * energy)), ou...]
    unnamed x2 -> x3, local copies, waits for them, and re-layouts: 2.43 us -> 3.99 us
    slice x1 -> x0, local copies, waits for them, and re-layouts: 1.26 us -> none  [per_device(): return (power, nyquist, mean[0])]
where the time goes in v2:
time: 82.9 us; the launch traced here: 82.7 us
  Pallas kernels  78.1 us (94%)
  local copies, waits for them, and re-layouts  3.99 us (5%)
    pallas_call x1, Pallas kernels, per_device(): pl.pallas_call(functools.partial(welch_kernel, 1.0 / (63.0 * energy)), ou...  78.1 us
    unnamed x3, local copies, waits for them, and re-layouts  3.99 us

profile of v2, /device:TPU:2, one launch (start us, length us, event | category | flops | bytes accessed | tf_op | source)
XLA Modules:
  0.0 82.7 jit_solution(8620171591015658068)
XLA Ops:
  0.6 78.1 %shard_map.112 = (f32[192,256]{1,0:T(8,128)}, f32[1,192]{1,0:T(1,128)}, f32[1,256]{1,0:T(1,128)}) custom-call(f32[24576,128]{1,0:T(8,128)} %bitcast.7, bf16[256,256]{1,0:T(8,128)(2,1)} %constant.16.clone.refs_0_, bf16[256,256]{1,0:T(8,128)(2,1)} %constant.17.clone.refs_1_, bf16[256,256]{1,0:T(8,128)(2,1)} %constant.18.clone.refs_2_, ...), custom_call_target="tpu_custom_call" | custom-call | tf_op jit(solution)/shard_map/pallas_call | solution.py:604
  78.7 1.6 %copy.15 = f32[192,256]{1,0:T(8,128)} copy(f32[192,256]{1,0:T(8,128)} %get-tuple-element.12) | data formatting | bytes 393216
  80.3 1.2 %copy.16 = f32[192]{0:T(256)} copy(f32[192]{0:T(256)} %bitcast.9) | data formatting | bytes 1536
  81.5 1.2 %copy.17 = f32[256]{0:T(256)} copy(f32[256]{0:T(256)} %bitcast.8) | data formatting | bytes 2048

commit v3 on v2

--- a/solution.py
+++ b/solution.py
@@ -13,7 +13,7 @@
 F32 = jnp.float32
 BF16 = jnp.bfloat16
 STRIDE = 8
-CHUNK = 2
+CHUNK = 4
 
 
 def split(values):
@@ -84,42 +84,41 @@
     return jnp.dot(a, b, preferred_element_type=F32)
 
 
-def first_stage(blocks, start, segs, ch, tabs, mean_ref, mean_base, mid_ref, high_ref, low_ref, row0):
+def first_stage(blocks, start, pair, ch, tabs, mean_ref, mean_base, mid_ref, mid_row, high_ref, low_ref):
     t_ref, vh_ref, vl_ref, c_ref, s_ref, mid_tw, w_ref = tabs
     w0, w1 = w_ref[:64, :], w_ref[64:, :]
     row = lax.broadcasted_iota(jnp.int32, (8, 256), 0)
-    for pair in range(segs // 2):
-        highs, lows = [], []
-        for s in (2 * pair, 2 * pair + 1):
-            mean = mean_ref[pl.ds(mean_base + s * 8 + ch, 1), :]
-            r0, b0, b1 = blocks, start + s * 512, start + s * 512 + 512
-            x0 = (r0[pl.ds(b0 + ch, 64, STRIDE), :] - mean) * w0
-            x1 = (r0[pl.ds(b1 + ch, 64, STRIDE), :] - mean) * w1
-            high, low = split(jnp.concatenate([x0, x1], 0))
-            highs.append(high)
-            lows.append(low)
-        x = jnp.concatenate(
-            [jnp.concatenate(highs, 1), jnp.concatenate(lows, 1)], 0
-        )
-        both = dot(t_ref[...], x)
-        d = both[:128] + both[128:]
-        fr = d[:64]
-        fi = jnp.concatenate([jnp.where(row == 0, 0.0, d[64:72]), d[72:]], 0)
-        mid = d[64:65]
-        c, s_ = c_ref[...], s_ref[...]
-        for i in range(2):
-            s = 2 * pair + i
-            lanes = slice(i * ROOT, (i + 1) * ROOT)
-            tr = fr[:, lanes] * c + fi[:, lanes] * s_
-            ti = fi[:, lanes] * c - fr[:, lanes] * s_
-            put = row0 + 64 * s
-            high, low = split(jnp.concatenate([tr, ti], 1))
-            high_ref[pl.ds(put, 64), :] = high
-            low_ref[pl.ds(put, 64), :] = low
-            m = mid[:, lanes]
-            mid_ref[pl.ds(mean_base + s * 8 + ch, 1), :] = jnp.concatenate(
-                [m * mid_tw[0:1, :], -m * mid_tw[1:2, :]], 1
-            )
+    highs, lows = [], []
+    for s in (2 * pair, 2 * pair + 1):
+        mean = mean_ref[pl.ds(mean_base + s * 8 + ch, 1), :]
+        r0, b0, b1 = blocks, start + s * 512, start + s * 512 + 512
+        x0 = (r0[pl.ds(b0 + ch, 64, STRIDE), :] - mean) * w0
+        x1 = (r0[pl.ds(b1 + ch, 64, STRIDE), :] - mean) * w1
+        high, low = split(jnp.concatenate([x0, x1], 0))
+        highs.append(high)
+        lows.append(low)
+    x = jnp.concatenate(
+        [jnp.concatenate(highs, 1), jnp.concatenate(lows, 1)], 0
+    )
+    both = dot(t_ref[...], x)
+    d = both[:128] + both[128:]
+    fr = d[:64]
+    fi = jnp.concatenate([jnp.where(row == 0, 0.0, d[64:72]), d[72:]], 0)
+    mid = d[64:65]
+    c, s_ = c_ref[...], s_ref[...]
+    for i in range(2):
+        s = 2 * pair + i
+        lanes = slice(i * ROOT, (i + 1) * ROOT)
+        tr = fr[:, lanes] * c + fi[:, lanes] * s_
+        ti = fi[:, lanes] * c - fr[:, lanes] * s_
+        put = ch * 128 + 64 * i
+        high, low = split(jnp.concatenate([tr, ti], 1))
+        high_ref[pl.ds(put, 64), :] = high
+        low_ref[pl.ds(put, 64), :] = low
+        m = mid[:, lanes]
+        mid_ref[pl.ds(mid_row + s * 8 + ch, 1), :] = jnp.concatenate(
+            [m * mid_tw[0:1, :], -m * mid_tw[1:2, :]], 1
+        )
 
 
 def squares(high, low, vh_ref, vl_ref):
@@ -135,13 +134,13 @@
 AHEAD = 2
 
 
-def remote(src, dst, send, recv, axis, index):
+def remote(src, dst, send, recv, axis, index, **more):
     return pltpu.make_async_remote_copy(
         src_ref=src,
         dst_ref=dst,
         send_sem=send,
         recv_sem=recv,
-        device_id={axis: index},
+        device_id={axis: index, **more},
         device_id_type=pl.DeviceIdType.MESH,
     )
 
@@ -172,7 +171,7 @@
     (relay, relay_send, relay_recv), refs = refs[3:6], refs[:3] + refs[6:]
     (buf, mean_ref, mid_ref, high_ref, low_ref, pow_ref) = refs[3:9]
     (zs, z_near, z_far, xs, x_near, x_far, allf) = refs[9:16]
-    (edge_z, edge_x, edge_sum, mean_buf) = refs[16:20]
+    (edge_z, edge_x, edge_sum, mean_buf, mean_sum), refs = refs[16:21], refs[:20] + refs[21:]
     (load_sem, pair_send, pair_recv, halo_send, halo_recv, z_send, z_recv) = refs[20:27]
     (x_send, x_recv, d_send, d_recv, e_send, e_recv, m_send, m_recv) = refs[27:]
     y = lax.axis_index("chan")
@@ -219,7 +218,7 @@
             target * 2 + core,
         )
 
-    def hop(g, half):
+    def hop(g, half, to):
         here = entry(g, half) + half * 4 * HALF_ROWS
         return remote(
             buf.at[pl.ds(here, HALF_ROWS), :],
@@ -227,11 +226,10 @@
             halo_send.at[g, half],
             relay_recv.at[g],
             "tm",
-            device(lax.rem(z + (3 if half == 0 else 1), 4), x, core),
-        )
-
-    def onward(g):
-        half = x // 3
+            to,
+        )
+
+    def onward(g, half, to):
         there = entry(g, half) + (1 - half) * 4 * HALF_ROWS
         return remote(
             relay.at[pl.ds(g * HALF_ROWS, HALF_ROWS), :],
@@ -239,10 +237,12 @@
             relay_send.at[g],
             halo_recv.at[g, half],
             "tm",
-            device(z, 3 - x, core),
+            to,
         )
 
     relays = (core == 1) & ((x == 0) | (x == 3))
+    relay_half = x // 3
+    relay_to = device(z, 3 - x, core)
 
     def z_copy(g, way, step):
         near, far = partners(z, way)
@@ -295,9 +295,10 @@
         )
 
     def mean_copy(step):
+        target = core if step % 2 == 0 else other
         return remote(
             mean_buf.at[0], mean_buf.at[step], m_send.at[step], m_recv.at[step],
-            "chan", lax.rem(y + step, 4),
+            "tm", device(z, x, target), chan=lax.rem(y + step // 2, 4),
         )
 
     def z_first(g):
@@ -342,60 +343,80 @@
             x_copy(b, way, 1).wait_recv()
             at = place(x, way)
             total = xs[way, b, at] + x_near[way, b, at - keep(x, way)] + x_far[way, b, 0]
+            both = total[0] + total[1]
+            column = both[:, :ROOT] + both[:, ROOT : 2 * ROOT]
+            column = column + (both[:, 2 * ROOT : 3 * ROOT] + both[:, 3 * ROOT :])
+            mean_buf[0] = mean_buf[0] + column
             for k in range(2):
                 for i in range(4):
                     row = pl.multiple_of(b * 128 + k * 64 + (way * 4 + i) * 8, 8)
                     allf[core, pl.ds(row, 8), :] = total[k, :, i * ROOT : (i + 1) * ROOT]
         d_copy(b, core).start()
 
+        @pl.when(b == BATCHES - 1)
+        def _():
+            for s in range(1, 8):
+                mean_copy(s).start()
+
     lane = lax.broadcasted_iota(jnp.int32, (8, ROOT), 1)
     sub = lax.broadcasted_iota(jnp.int32, (8, ROOT), 0)
 
-    def compute(g):
+    def phase(g, late):
         for half in range(2):
+            pair_index = (1 - half) if late else half
             first = pl.multiple_of(entry(g, half), 8)
-            halo(g, half).wait_recv()
+            if late:
+                halo(g, half).wait_recv()
             sums = []
-            for i in range(5):
+            for i in range(2 * pair_index, 2 * pair_index + 3):
                 rows = buf[pl.ds(pl.multiple_of(first + i * HALF_ROWS, 8), HALF_ROWS), :]
                 rows = rows.reshape(64, 8, ROOT)
                 sums.append(jnp.sum(jnp.sum(rows, axis=0), axis=1, keepdims=True))
             base = half * 32
-            for s in range(SEGS):
-                mean = (sums[s] + sums[s + 1]) * (1.0 / SEG)
-                mean_ref[base + s * 8 : base + s * 8 + 8, :] = jnp.broadcast_to(mean, (8, ROOT))
-            absent = (chip == 15, 3) if half == 0 else (chip == 0, 0)
+            for i in range(2):
+                mean = (sums[i] + sums[i + 1]) * (1.0 / SEG)
+                at = base + (2 * pair_index + i) * 8
+                mean_ref[at : at + 8, :] = jnp.broadcast_to(mean, (8, ROOT))
+            mid_row = pl.multiple_of(g * 64 + base, 8)
             for ch in range(8):
                 first_stage(
-                    buf, first, SEGS, ch, tabs, mean_ref, base, mid_ref, high_ref, low_ref, ch * 256
+                    buf, first, pair_index, ch, tabs, mean_ref, base, mid_ref, mid_row, high_ref, low_ref
                 )
+            gone = (chip == 15) if half == 0 else (chip == 0)
             for c0 in range(0, 8, CHUNK):
-                sl = slice(c0 * 256, (c0 + CHUNK) * 256)
+                sl = slice(c0 * 128, (c0 + CHUNK) * 128)
                 sq = squares(high_ref[sl, :], low_ref[sl, :], tabs[1], tabs[2])
                 for ch in range(c0, c0 + CHUNK):
-                    power = jnp.zeros((64, ROOT), F32)
-                    for s in range(SEGS):
-                        r = (ch - c0) * 256 + s * 64
-                        sqs = sq[r : r + 64]
-                        if s == absent[1]:
-                            sqs = jnp.where(absent[0], 0.0, sqs)
-                        power = power + sqs
-                    at = ch * 128 + 64 * half
-                    pow_ref[at : at + 64, :] = power
-            sq = squares(*split(mid_ref[base : base + 32, :]), tabs[1], tabs[2])
+                    r = (ch - c0) * 128
+                    one, two = sq[r : r + 64], sq[r + 64 : r + 128]
+                    at = pl.multiple_of(g * 1024 + ch * 128 + 64 * half, 64)
+                    if late:
+                        if half == 0:
+                            two = jnp.where(gone, 0.0, two)
+                        else:
+                            one = jnp.where(gone, 0.0, one)
+                        pow_ref[pl.ds(at, 64), :] = pow_ref[pl.ds(at, 64), :] + (one + two)
+                    else:
+                        pow_ref[pl.ds(at, 64), :] = one + two
+            if not late:
+                continue
+            sq = squares(*split(mid_ref[pl.ds(mid_row, 32), :]), tabs[1], tabs[2])
             middle = jnp.zeros((8, ROOT), F32)
             for s in range(SEGS):
                 sqs = sq[s * 8 : s * 8 + 8]
-                if s == absent[1]:
-                    sqs = jnp.where(absent[0], 0.0, sqs)
+                if s == 3 * (1 - half):
+                    sqs = jnp.where(gone, 0.0, sqs)
                 middle = middle + sqs
-            zero = pow_ref[pl.ds(64 * half, 8, 128), :]
+            zeros = pl.ds(g * 1024 + 64 * half, 8, 128)
+            zero = pow_ref[zeros, :]
             last = jnp.sum(jnp.where(lane == ROOT - 1, zero, 0.0), axis=1, keepdims=True)
             spot = lane == 48 * half + 8 * g + sub
             edge_z[0] = jnp.where(spot, jnp.broadcast_to(last, (8, ROOT)), edge_z[0])
-            pow_ref[pl.ds(64 * half, 8, 128), :] = jnp.where(lax.rem(lane, 4) >= 2, middle, zero)
+            pow_ref[zeros, :] = jnp.where(lax.rem(lane, 4) >= 2, middle, zero)
+        if not late:
+            return
         for i in range(8):
-            block = pow_ref[i * 128 : (i + 1) * 128, :].T
+            block = pow_ref[pl.ds(pl.multiple_of(g * 1024 + i * 128, 128), 128), :].T
             lanes = slice((i % 4) * ROOT, (i % 4 + 1) * ROOT)
             for chunk in range(4):
                 spot = ((0, 2, 3, 1)[chunk] if i < 4 else chunk) * 32
@@ -419,24 +440,30 @@
     peers = [("tm", device(z, x, other))]
     for step in (1, 15):
         peers.append(("tm", lax.rem(chip + step, 16) * 2 + core))
-    for step in (1, 2, 3):
+    for step in (1, 3):
         peers.append(("tm", device(lax.rem(z + step, 4), x, core)))
         peers.append(("tm", device(z, lax.rem(x + step, 4), core)))
-        peers.append(("chan", lax.rem(y + step, 4)))
-    for axis, index in peers:
+    peers.append(("tm", device(lax.rem(z + 2, 4), x, core)))
+    peers.append(("tm", device(z, lax.rem(x + 2, 4), core)))
+    signals = [{axis: index} for axis, index in peers]
+    for step in (1, 2, 3):
+        for to in (core, other):
+            signals.append({"chan": lax.rem(y + step, 4), "tm": device(z, x, to)})
+    for to in signals:
         pl.semaphore_signal(
-            barrier, inc=1, device_id={axis: index}, device_id_type=pl.DeviceIdType.MESH
-        )
-    pl.semaphore_wait(barrier, len(peers))
+            barrier, inc=1, device_id=to, device_id_type=pl.DeviceIdType.MESH
+        )
+    pl.semaphore_wait(barrier, len(signals))
     def arrived(g):
         for half in range(2):
             load(g, half).wait()
             pair_arrival(g, half).wait_recv()
             by_relay = (core == 1) & (x == 3 * half)
+            to = device(lax.rem(z + 3 + 2 * half, 4), x, core)
 
             @pl.when(by_relay)
             def _():
-                hop(g, half).start()
+                hop(g, half, to).start()
 
             @pl.when(jnp.logical_not(by_relay))
             def _():
@@ -445,16 +472,19 @@
     def forward(g):
         @pl.when(relays)
         def _():
-            hop(g, 0).wait_recv()
-            onward(g).start()
+            hop(g, 0, relay_to).wait_recv()
+            onward(g, relay_half, relay_to).start()
 
     for g in range(AHEAD + 1):
         for half in range(2):
             pair(g, half).start()
     edge_z[0] = jnp.zeros((8, ROOT), F32)
+    mean_buf[0] = jnp.zeros((8, ROOT), F32)
     for g in range(AHEAD):
         arrived(g)
+    phase(0, False)
     forward(0)
+    phase(1, False)
 
     def step(g, carry):
         @pl.when(g < GROUPS - AHEAD - 1)
@@ -470,9 +500,13 @@
         def _():
             forward(g + 1)
 
+        @pl.when(g < GROUPS - 2)
+        def _():
+            phase(g + 2, False)
+
         @pl.when(g < GROUPS)
         def _():
-            compute(g)
+            phase(g, True)
             z_first(g)
 
         @pl.when(g == GROUPS - 1)
@@ -524,15 +558,22 @@
     lax.fori_loop(0, GROUPS + 4, step, 0)
     for b in range(BATCHES):
         d_copy(b, other).wait_recv()
+    total = mean_buf[0]
+    for s in range(1, 8):
+        mean_copy(s).wait_recv()
+        total = total + mean_buf[s]
+    mean_sum[...] = total
     lane_row = lax.broadcasted_iota(jnp.int32, (1, ROOT), 1)
-    pieces = []
     for par in range(2):
         stacked = []
         for h in range(2):
             near = allf[h, pl.ds(4 * core + par, 48, 8), :]
             far = allf[h, pl.ds(4 * core + par + 2, 48, 8), :]
             stacked.append(jnp.concatenate([near, far], 1))
-        value = jnp.concatenate(stacked, 0)
+        row = jnp.concatenate(
+            [mean_sum[pl.ds(4 * core + par, 1), :], mean_sum[pl.ds(4 * core + par + 2, 1), :]], 1
+        )
+        value = jnp.concatenate(stacked + [jnp.broadcast_to(row, (8, 256))], 0)
         high, rest = split(value)
         low = rest.astype(F32)
         rest = (value - high.astype(F32)) - low
@@ -546,14 +587,8 @@
             for h in range(2):
                 at = h * 96 + kind * 48
                 power_out[at : at + 48, par * ROOT : (par + 1) * ROOT] = out[h * 48 : h * 48 + 48]
-            pieces.append(out)
-    sums = []
-    for par in range(2):
-        both = pieces[2 * par] + pieces[2 * par + 1]
-        sums.append(jnp.sum(both, axis=0, keepdims=True))
-    mean_buf[0] = jnp.broadcast_to(jnp.concatenate(sums, 1), (8, 256))
-    for s in (1, 2, 3):
-        mean_copy(s).start()
+        row = (placed[96:97, :ROOT] + placed[96:97, ROOT:]) * factor
+        mean_out[:, par * ROOT : (par + 1) * ROOT] = row * (1.0 / 768.0)
 
     def drain(g, carry):
         for way in range(2):
@@ -564,7 +599,7 @@
 
         @pl.when(relays)
         def _():
-            onward(g).wait_send()
+            onward(g, relay_half, relay_to).wait_send()
 
         return carry
 
@@ -583,12 +618,7 @@
         mine = jnp.where(core == h, edge_sum[0], edge_sum[1])
         row = jnp.sum(mine, axis=0, keepdims=True) * scale
         edge_out[:, h * 96 : h * 96 + 96] = row[:, :96]
-    mean = mean_buf[0]
-    for s in (1, 2, 3):
-        mean_copy(s).wait_recv()
-        mean = mean + mean_buf[s]
-    mean_out[...] = mean[:1] * (1.0 / 768.0)
-    for s in (1, 2, 3):
+    for s in range(1, 8):
         mean_copy(s).wait_send()
 
 
@@ -616,10 +646,10 @@
             dma((GROUPS,)),
             pltpu.VMEM((GROUPS * 2 * ENTRY_ROWS, ROOT), F32),
             pltpu.VMEM((64, ROOT), F32),
-            pltpu.VMEM((64, 256), F32),
-            pltpu.VMEM((2048, 256), BF16),
-            pltpu.VMEM((2048, 256), BF16),
-            pltpu.VMEM((1024, ROOT), F32),
+            pltpu.VMEM((GROUPS * 64, 256), F32),
+            pltpu.VMEM((1024, 256), BF16),
+            pltpu.VMEM((1024, 256), BF16),
+            pltpu.VMEM((GROUPS * 1024, ROOT), F32),
             pltpu.VMEM((2, GROUPS, 128, 512), F32),
             pltpu.VMEM((2, GROUPS, 64, 512), F32),
             pltpu.VMEM((2, GROUPS, 32, 512), F32),
@@ -630,7 +660,8 @@
             pltpu.VMEM((4, 8, ROOT), F32),
             pltpu.VMEM((4, 8, ROOT), F32),
             pltpu.VMEM((2, 8, ROOT), F32),
-            pltpu.VMEM((4, 8, 256), F32),
+            pltpu.VMEM((8, 8, ROOT), F32),
+            pltpu.VMEM((8, ROOT), F32),
             dma((GROUPS, 2)),
             dma((GROUPS, 2)),
             dma((GROUPS, 2)),
@@ -644,8 +675,8 @@
             dma((BATCHES,)),
             dma((3, 4)),
             dma((3, 4)),
-            dma((4,)),
-            dma((4,)),
+            dma((8,)),
+            dma((8,)),
         ],
         compiler_params=pltpu.CompilerParams(
             collective_id=0, has_side_effects=True, vmem_limit_bytes=60 * 1024 * 1024

time: 82.9 us -> 80.1 us (0.966)
  Pallas kernels: 78.1 us -> 75 us
    pallas_call x1, Pallas kernels: 78.1 us -> 75 us  [per_device(): pl.pallas_call(functools.partial(welch_kernel, 1.0 / (63.0 * energy)), ou...]
where the time goes in v3:
time: 80.1 us; the launch traced here: 79.6 us
  Pallas kernels  75 us (94%)
  local copies, waits for them, and re-layouts  3.99 us (5%)
    pallas_call x1, Pallas kernels, per_device(): pl.pallas_call(functools.partial(welch_kernel, 1.0 / (63.0 * energy)), ou...  75 us
    unnamed x3, local copies, waits for them, and re-layouts  3.99 us

profile of v3, /device:TPU:2, one launch (start us, length us, event | category | flops | bytes accessed | tf_op | source)
XLA Modules:
  0.0 79.6 jit_solution(12202905265635936565)
XLA Ops:
  0.6 75.0 %shard_map.112 = (f32[192,256]{1,0:T(8,128)}, f32[1,192]{1,0:T(1,128)}, f32[1,256]{1,0:T(1,128)}) custom-call(f32[24576,128]{1,0:T(8,128)} %bitcast.7, bf16[256,256]{1,0:T(8,128)(2,1)} %constant.16.clone.refs_0_, bf16[256,256]{1,0:T(8,128)(2,1)} %constant.17.clone.refs_1_, bf16[256,256]{1,0:T(8,128)(2,1)} %constant.18.clone.refs_2_, ...), custom_call_target="tpu_custom_call" | custom-call | tf_op jit(solution)/shard_map/pallas_call | solution.py:634
  75.6 1.6 %copy.15 = f32[192,256]{1,0:T(8,128)} copy(f32[192,256]{1,0:T(8,128)} %get-tuple-element.12) | data formatting | bytes 393216
  77.3 1.2 %copy.16 = f32[192]{0:T(256)} copy(f32[192]{0:T(256)} %bitcast.9) | data formatting | bytes 1536
  78.4 1.2 %copy.17 = f32[256]{0:T(256)} copy(f32[256]{0:T(256)} %bitcast.8) | data formatting | bytes 2048

commit v4 on v3

--- a/solution.py
+++ b/solution.py
@@ -130,7 +130,8 @@
 HALF_ROWS = 512
 ENTRY_ROWS = 5 * HALF_ROWS
 SEGS = 4
-BATCHES = 3
+ENTRIES = 2 * GROUPS
+BATCHES = GROUPS
 AHEAD = 2
 
 
@@ -168,7 +169,7 @@
 def welch_kernel(scale, x_ref, *refs):
     tabs, perm_ref, refs = refs[:7], refs[7], refs[8:]
     power_out, edge_out, mean_out = refs[:3]
-    (relay, relay_send, relay_recv), refs = refs[3:6], refs[:3] + refs[6:]
+    (relay, relay_send, relay_recv, spread), refs = refs[3:7], refs[:3] + refs[7:]
     (buf, mean_ref, mid_ref, high_ref, low_ref, pow_ref) = refs[3:9]
     (zs, z_near, z_far, xs, x_near, x_far, allf) = refs[9:16]
     (edge_z, edge_x, edge_sum, mean_buf, mean_sum), refs = refs[16:21], refs[:20] + refs[21:]
@@ -274,9 +275,11 @@
             device(z, to, core),
         )
 
-    def d_copy(b, half_owner):
-        rows = allf.at[half_owner, pl.ds(b * 128, 128), :]
-        return remote(rows, rows, d_send.at[b], d_recv.at[b], "tm", device(z, x, other))
+    def d_copy(b, half, half_owner):
+        rows = allf.at[half_owner, pl.ds(half * 192 + b * 32, 32), :]
+        return remote(
+            rows, rows, d_send.at[b, half], d_recv.at[b, half], "tm", device(z, x, other)
+        )
 
     def edge_copy(stage, step):
         if stage == 0:
@@ -344,14 +347,13 @@
             at = place(x, way)
             total = xs[way, b, at] + x_near[way, b, at - keep(x, way)] + x_far[way, b, 0]
             both = total[0] + total[1]
-            column = both[:, :ROOT] + both[:, ROOT : 2 * ROOT]
-            column = column + (both[:, 2 * ROOT : 3 * ROOT] + both[:, 3 * ROOT :])
-            mean_buf[0] = mean_buf[0] + column
+            mean_buf[0] = mean_buf[0] + (both[:, :ROOT] + both[:, ROOT:])
             for k in range(2):
-                for i in range(4):
-                    row = pl.multiple_of(b * 128 + k * 64 + (way * 4 + i) * 8, 8)
+                for i in range(2):
+                    row = pl.multiple_of(k * 192 + b * 32 + (way * 2 + i) * 8, 8)
                     allf[core, pl.ds(row, 8), :] = total[k, :, i * ROOT : (i + 1) * ROOT]
-        d_copy(b, core).start()
+        for k in range(2):
+            d_copy(b, k, core).start()
 
         @pl.when(b == BATCHES - 1)
         def _():
@@ -361,66 +363,65 @@
     lane = lax.broadcasted_iota(jnp.int32, (8, ROOT), 1)
     sub = lax.broadcasted_iota(jnp.int32, (8, ROOT), 0)
 
-    def phase(g, late):
-        for half in range(2):
-            pair_index = (1 - half) if late else half
-            first = pl.multiple_of(entry(g, half), 8)
-            if late:
-                halo(g, half).wait_recv()
-            sums = []
-            for i in range(2 * pair_index, 2 * pair_index + 3):
-                rows = buf[pl.ds(pl.multiple_of(first + i * HALF_ROWS, 8), HALF_ROWS), :]
-                rows = rows.reshape(64, 8, ROOT)
-                sums.append(jnp.sum(jnp.sum(rows, axis=0), axis=1, keepdims=True))
-            base = half * 32
-            for i in range(2):
-                mean = (sums[i] + sums[i + 1]) * (1.0 / SEG)
-                at = base + (2 * pair_index + i) * 8
-                mean_ref[at : at + 8, :] = jnp.broadcast_to(mean, (8, ROOT))
-            mid_row = pl.multiple_of(g * 64 + base, 8)
-            for ch in range(8):
-                first_stage(
-                    buf, first, pair_index, ch, tabs, mean_ref, base, mid_ref, mid_row, high_ref, low_ref
-                )
-            gone = (chip == 15) if half == 0 else (chip == 0)
-            for c0 in range(0, 8, CHUNK):
-                sl = slice(c0 * 128, (c0 + CHUNK) * 128)
-                sq = squares(high_ref[sl, :], low_ref[sl, :], tabs[1], tabs[2])
-                for ch in range(c0, c0 + CHUNK):
-                    r = (ch - c0) * 128
-                    one, two = sq[r : r + 64], sq[r + 64 : r + 128]
-                    at = pl.multiple_of(g * 1024 + ch * 128 + 64 * half, 64)
-                    if late:
-                        if half == 0:
-                            two = jnp.where(gone, 0.0, two)
-                        else:
-                            one = jnp.where(gone, 0.0, one)
-                        pow_ref[pl.ds(at, 64), :] = pow_ref[pl.ds(at, 64), :] + (one + two)
+    def phase(g, half, late):
+        pair_index = (1 - half) if late else half
+        first = pl.multiple_of(entry(g, half), 8)
+        if late:
+            halo(g, half).wait_recv()
+        sums = []
+        for i in range(2 * pair_index, 2 * pair_index + 3):
+            rows = buf[pl.ds(pl.multiple_of(first + i * HALF_ROWS, 8), HALF_ROWS), :]
+            rows = rows.reshape(64, 8, ROOT)
+            sums.append(jnp.sum(jnp.sum(rows, axis=0), axis=1, keepdims=True))
+        base = half * 32
+        for i in range(2):
+            mean = (sums[i] + sums[i + 1]) * (1.0 / SEG)
+            at = base + (2 * pair_index + i) * 8
+            mean_ref[at : at + 8, :] = jnp.broadcast_to(mean, (8, ROOT))
+        mid_row = pl.multiple_of(g * 64 + base, 8)
+        for ch in range(8):
+            first_stage(
+                buf, first, pair_index, ch, tabs, mean_ref, base, mid_ref, mid_row, high_ref, low_ref
+            )
+        gone = (chip == 15) if half == 0 else (chip == 0)
+        for c0 in range(0, 8, CHUNK):
+            sl = slice(c0 * 128, (c0 + CHUNK) * 128)
+            sq = squares(high_ref[sl, :], low_ref[sl, :], tabs[1], tabs[2])
+            for ch in range(c0, c0 + CHUNK):
+                r = (ch - c0) * 128
+                one, two = sq[r : r + 64], sq[r + 64 : r + 128]
+                at = pl.multiple_of(g * 1024 + half * 512 + ch * 64, 64)
+                if late:
+                    if half == 0:
+                        two = jnp.where(gone, 0.0, two)
                     else:
-                        pow_ref[pl.ds(at, 64), :] = one + two
-            if not late:
-                continue
-            sq = squares(*split(mid_ref[pl.ds(mid_row, 32), :]), tabs[1], tabs[2])
-            middle = jnp.zeros((8, ROOT), F32)
-            for s in range(SEGS):
-                sqs = sq[s * 8 : s * 8 + 8]
-                if s == 3 * (1 - half):
-                    sqs = jnp.where(gone, 0.0, sqs)
-                middle = middle + sqs
-            zeros = pl.ds(g * 1024 + 64 * half, 8, 128)
-            zero = pow_ref[zeros, :]
-            last = jnp.sum(jnp.where(lane == ROOT - 1, zero, 0.0), axis=1, keepdims=True)
-            spot = lane == 48 * half + 8 * g + sub
-            edge_z[0] = jnp.where(spot, jnp.broadcast_to(last, (8, ROOT)), edge_z[0])
-            pow_ref[zeros, :] = jnp.where(lax.rem(lane, 4) >= 2, middle, zero)
+                        one = jnp.where(gone, 0.0, one)
+                    pow_ref[pl.ds(at, 64), :] = pow_ref[pl.ds(at, 64), :] + (one + two)
+                else:
+                    pow_ref[pl.ds(at, 64), :] = one + two
         if not late:
             return
-        for i in range(8):
-            block = pow_ref[pl.ds(pl.multiple_of(g * 1024 + i * 128, 128), 128), :].T
-            lanes = slice((i % 4) * ROOT, (i % 4 + 1) * ROOT)
+        sq = squares(*split(mid_ref[pl.ds(mid_row, 32), :]), tabs[1], tabs[2])
+        middle = jnp.zeros((8, ROOT), F32)
+        for s in range(SEGS):
+            sqs = sq[s * 8 : s * 8 + 8]
+            if s == 3 * (1 - half):
+                sqs = jnp.where(gone, 0.0, sqs)
+            middle = middle + sqs
+        zeros = pl.ds(g * 1024 + half * 512, 8, 64)
+        zero = pow_ref[zeros, :]
+        last = jnp.sum(jnp.where(lane == ROOT - 1, zero, 0.0), axis=1, keepdims=True)
+        spot = lane == 48 * half + 8 * g + sub
+        edge_z[0] = jnp.where(spot, jnp.broadcast_to(last, (8, ROOT)), edge_z[0])
+        pow_ref[zeros, :] = jnp.where(lax.rem(lane, 4) >= 2, middle, zero)
+        for i in range(4):
+            block = pow_ref[pl.ds(pl.multiple_of(g * 1024 + half * 512 + i * 128, 128), 128), :].T
+            lanes = slice((i % 2) * ROOT, (i % 2 + 1) * ROOT)
             for chunk in range(4):
-                spot = ((0, 2, 3, 1)[chunk] if i < 4 else chunk) * 32
-                zs[i // 4, g, spot : spot + 32, lanes] = block[chunk * 32 : chunk * 32 + 32]
+                spot = ((0, 2, 3, 1)[chunk] if i < 2 else chunk) * 32
+                zs[i // 2, 2 * g + half, spot : spot + 32, lanes] = block[
+                    chunk * 32 : chunk * 32 + 32
+                ]
 
     def pair_arrival(g, half):
         to = entry(g, half) + (2 * other + half) * HALF_ROWS
@@ -482,9 +483,9 @@
     mean_buf[0] = jnp.zeros((8, ROOT), F32)
     for g in range(AHEAD):
         arrived(g)
-    phase(0, False)
+    for half in range(2):
+        phase(0, half, False)
     forward(0)
-    phase(1, False)
 
     def step(g, carry):
         @pl.when(g < GROUPS - AHEAD - 1)
@@ -500,41 +501,48 @@
         def _():
             forward(g + 1)
 
-        @pl.when(g < GROUPS - 2)
-        def _():
-            phase(g + 2, False)
-
-        @pl.when(g < GROUPS)
-        def _():
-            phase(g, True)
-            z_first(g)
-
-        @pl.when(g == GROUPS - 1)
-        def _():
-            for s in (1, 2, 3):
-                edge_copy(0, s).start()
-
-        @pl.when((g >= 1) & (g < GROUPS + 1))
-        def _():
-            z_second(g - 1)
-
-        @pl.when((g >= 2) & (g < GROUPS + 2))
-        def _():
-            z_last(g - 2)
-
-        @pl.when((g >= 3) & (g < GROUPS + 2) & (lax.rem(g, 2) == 1))
-        def _():
-            x_first((g - 3) // 2)
-
-        @pl.when((g >= 4) & (g < GROUPS + 3) & (lax.rem(g, 2) == 0))
-        def _():
-            x_second((g - 4) // 2)
-
-        @pl.when((g >= 5) & (lax.rem(g, 2) == 1))
-        def _():
-            to_pair((g - 5) // 2)
-
-        @pl.when(g == GROUPS + 1)
+        for half in range(2):
+            entry_now = 2 * g + half
+
+            @pl.when(g < GROUPS - 1)
+            def _():
+                phase(g + 1, half, False)
+
+            @pl.when(g < GROUPS)
+            def _():
+                phase(g, half, True)
+                z_first(entry_now)
+
+            if half == 1:
+
+                @pl.when(g == GROUPS - 1)
+                def _():
+                    for s in (1, 2, 3):
+                        edge_copy(0, s).start()
+
+            @pl.when((entry_now >= 2) & (entry_now < ENTRIES + 2))
+            def _():
+                z_second(entry_now - 2)
+
+            @pl.when((entry_now >= 4) & (entry_now < ENTRIES + 4))
+            def _():
+                z_last(entry_now - 4)
+
+            if half == 1:
+
+                @pl.when((g >= 2) & (g < GROUPS + 2))
+                def _():
+                    x_first(g - 2)
+
+                @pl.when((g >= 3) & (g < GROUPS + 3))
+                def _():
+                    x_second(g - 3)
+
+                @pl.when(g >= 4)
+                def _():
+                    to_pair(g - 4)
+
+        @pl.when(g == GROUPS)
         def _():
             total = edge_z[0]
             for s in (1, 2, 3):
@@ -544,7 +552,7 @@
             for s in (1, 2, 3):
                 edge_copy(1, s).start()
 
-        @pl.when(g == GROUPS + 3)
+        @pl.when(g == GROUPS + 1)
         def _():
             total = edge_x[0]
             for s in (1, 2, 3):
@@ -557,7 +565,8 @@
 
     lax.fori_loop(0, GROUPS + 4, step, 0)
     for b in range(BATCHES):
-        d_copy(b, other).wait_recv()
+        for k in range(2):
+            d_copy(b, k, other).wait_recv()
     total = mean_buf[0]
     for s in range(1, 8):
         mean_copy(s).wait_recv()
@@ -585,15 +594,20 @@
         for kind in range(2):
             out = placed[:, kind * ROOT : (kind + 1) * ROOT] * factor
             for h in range(2):
-                at = h * 96 + kind * 48
-                power_out[at : at + 48, par * ROOT : (par + 1) * ROOT] = out[h * 48 : h * 48 + 48]
+                for half in range(2):
+                    at = h * 96 + half * 48 + kind
+                    spread[par, pl.ds(at, 24, 2), :] = out[
+                        h * 48 + half * 24 : h * 48 + half * 24 + 24
+                    ]
+        power_out[:, par * ROOT : (par + 1) * ROOT] = spread[par]
         row = (placed[96:97, :ROOT] + placed[96:97, ROOT:]) * factor
         mean_out[:, par * ROOT : (par + 1) * ROOT] = row * (1.0 / 768.0)
 
     def drain(g, carry):
         for way in range(2):
             for step in range(2):
-                z_copy(g, way, step).wait_send()
+                z_copy(2 * g, way, step).wait_send()
+                z_copy(2 * g + 1, way, step).wait_send()
             pair(g, way).wait_send()
             halo(g, way).wait_send()
 
@@ -608,7 +622,8 @@
         for way in range(2):
             for step in range(2):
                 x_copy(b, way, step).wait_send()
-        d_copy(b, core).wait_send()
+        for k in range(2):
+            d_copy(b, k, core).wait_send()
     for s in (1, 2, 3):
         edge_copy(0, s).wait_send()
         edge_copy(1, s).wait_send()
@@ -644,18 +659,19 @@
             pltpu.VMEM((GROUPS * HALF_ROWS, ROOT), F32),
             dma((GROUPS,)),
             dma((GROUPS,)),
+            pltpu.VMEM((2, 192, ROOT), F32),
             pltpu.VMEM((GROUPS * 2 * ENTRY_ROWS, ROOT), F32),
             pltpu.VMEM((64, ROOT), F32),
             pltpu.VMEM((GROUPS * 64, 256), F32),
             pltpu.VMEM((1024, 256), BF16),
             pltpu.VMEM((1024, 256), BF16),
             pltpu.VMEM((GROUPS * 1024, ROOT), F32),
-            pltpu.VMEM((2, GROUPS, 128, 512), F32),
-            pltpu.VMEM((2, GROUPS, 64, 512), F32),
-            pltpu.VMEM((2, GROUPS, 32, 512), F32),
-            pltpu.VMEM((2, BATCHES, 4, 2, 8, 512), F32),
-            pltpu.VMEM((2, BATCHES, 2, 2, 8, 512), F32),
-            pltpu.VMEM((2, BATCHES, 1, 2, 8, 512), F32),
+            pltpu.VMEM((2, ENTRIES, 128, 256), F32),
+            pltpu.VMEM((2, ENTRIES, 64, 256), F32),
+            pltpu.VMEM((2, ENTRIES, 32, 256), F32),
+            pltpu.VMEM((2, BATCHES, 4, 2, 8, 256), F32),
+            pltpu.VMEM((2, BATCHES, 2, 2, 8, 256), F32),
+            pltpu.VMEM((2, BATCHES, 1, 2, 8, 256), F32),
             pltpu.VMEM((2, GROUPS * 64, ROOT), F32),
             pltpu.VMEM((4, 8, ROOT), F32),
             pltpu.VMEM((4, 8, ROOT), F32),
@@ -667,12 +683,12 @@
             dma((GROUPS, 2)),
             dma((GROUPS, 2)),
             dma((GROUPS, 2)),
-            dma((2, GROUPS, 2)),
-            dma((2, GROUPS, 2)),
+            dma((2, ENTRIES, 2)),
+            dma((2, ENTRIES, 2)),
             dma((2, BATCHES, 2)),
             dma((2, BATCHES, 2)),
-            dma((BATCHES,)),
-            dma((BATCHES,)),
+            dma((BATCHES, 2)),
+            dma((BATCHES, 2)),
             dma((3, 4)),
             dma((3, 4)),
             dma((8,)),

time: 80.1 us -> 78.5 us (0.980)
  Pallas kernels: 75 us -> 72.8 us
    pallas_call x1, Pallas kernels: 75 us -> 72.8 us  [per_device(): pl.pallas_call(functools.partial(welch_kernel, 1.0 / (63.0 * energy)), ou...]
where the time goes in v4:
time: 78.5 us; the launch traced here: 77.4 us
  Pallas kernels  72.8 us (93%)
  local copies, waits for them, and re-layouts  3.99 us (5%)
    pallas_call x1, Pallas kernels, per_device(): pl.pallas_call(functools.partial(welch_kernel, 1.0 / (63.0 * energy)), ou...  72.8 us
    unnamed x3, local copies, waits for them, and re-layouts  3.99 us

profile of v4, /device:TPU:2, one launch (start us, length us, event | category | flops | bytes accessed | tf_op | source)
XLA Modules:
  0.0 77.4 jit_solution(12046173331990262166)
XLA Ops:
  0.6 72.8 %shard_map.112 = (f32[192,256]{1,0:T(8,128)}, f32[1,192]{1,0:T(1,128)}, f32[1,256]{1,0:T(1,128)}) custom-call(f32[24576,128]{1,0:T(8,128)} %bitcast.7, bf16[256,256]{1,0:T(8,128)(2,1)} %constant.16.clone.refs_0_, bf16[256,256]{1,0:T(8,128)(2,1)} %constant.17.clone.refs_1_, bf16[256,256]{1,0:T(8,128)(2,1)} %constant.18.clone.refs_2_, ...), custom_call_target="tpu_custom_call" | custom-call | tf_op jit(solution)/shard_map/pallas_call | solution.py:649
  73.4 1.6 %copy.15 = f32[192,256]{1,0:T(8,128)} copy(f32[192,256]{1,0:T(8,128)} %get-tuple-element.12) | data formatting | bytes 393216
  75.0 1.2 %copy.16 = f32[192]{0:T(256)} copy(f32[192]{0:T(256)} %bitcast.9) | data formatting | bytes 1536
  76.2 1.2 %copy.17 = f32[256]{0:T(256)} copy(f32[256]{0:T(256)} %bitcast.8) | data formatting | bytes 2048

commit v5 on v4

--- a/solution.py
+++ b/solution.py
@@ -13,7 +13,7 @@
 F32 = jnp.float32
 BF16 = jnp.bfloat16
 STRIDE = 8
-CHUNK = 4
+CHUNK = 8
 
 
 def split(values):
@@ -497,16 +497,18 @@
         def _():
             arrived(g + AHEAD)
 
-        @pl.when(g < GROUPS - 1)
-        def _():
-            forward(g + 1)
-
         for half in range(2):
             entry_now = 2 * g + half
 
             @pl.when(g < GROUPS - 1)
             def _():
                 phase(g + 1, half, False)
+
+            if half == 0:
+
+                @pl.when(g < GROUPS - 1)
+                def _():
+                    forward(g + 1)
 
             @pl.when(g < GROUPS)
             def _():

time: 78.5 us -> 77.9 us (level)
  no operation moved by 1% of the time
where the time goes in v5:
time: 77.9 us; the launch traced here: 76.9 us
  Pallas kernels  72.3 us (93%)
  local copies, waits for them, and re-layouts  3.99 us (5%)
    pallas_call x1, Pallas kernels, per_device(): pl.pallas_call(functools.partial(welch_kernel, 1.0 / (63.0 * energy)), ou...  72.3 us
    unnamed x3, local copies, waits for them, and re-layouts  3.99 us

profile of v5, /device:TPU:2, one launch (start us, length us, event | category | flops | bytes accessed | tf_op | source)
XLA Modules:
  0.0 76.9 jit_solution(5204821038685708285)
XLA Ops:
  0.6 72.3 %shard_map.112 = (f32[192,256]{1,0:T(8,128)}, f32[1,192]{1,0:T(1,128)}, f32[1,256]{1,0:T(1,128)}) custom-call(f32[24576,128]{1,0:T(8,128)} %bitcast.7, bf16[256,256]{1,0:T(8,128)(2,1)} %constant.16.clone.refs_0_, bf16[256,256]{1,0:T(8,128)(2,1)} %constant.17.clone.refs_1_, bf16[256,256]{1,0:T(8,128)(2,1)} %constant.18.clone.refs_2_, ...), custom_call_target="tpu_custom_call" | custom-call | tf_op jit(solution)/shard_map/pallas_call | solution.py:651
  72.9 1.6 %copy.15 = f32[192,256]{1,0:T(8,128)} copy(f32[192,256]{1,0:T(8,128)} %get-tuple-element.12) | data formatting | bytes 393216
  74.5 1.2 %copy.16 = f32[192]{0:T(256)} copy(f32[192]{0:T(256)} %bitcast.9) | data formatting | bytes 1536
  75.7 1.2 %copy.17 = f32[256]{0:T(256)} copy(f32[256]{0:T(256)} %bitcast.8) | data formatting | bytes 2048
